TPU v7x, 256 devices: a whole 4x4x8 slice. The times are simulated.
256 devices in a mesh: interval: 4 (over z_lo, core), rows: 64 (over z_hi, x, y).
Axes of the slice: x: 4, y: 4, z: 8 (z_hi: 4, z_lo: 2; z = z_hi * 2 + z_lo), core: 2. Of those that a mesh axis runs over, the one named last changes fastest.
Arguments:
- filtered: float32 [4, 64, 1048576], P('interval', None, 'rows'), may hold values from -60 to 60, as said below
- potential: float32 [128, 64, 128], P('rows'), may hold values from 0.5 to 4
Outputs:
- basis: float32 [4, 64, 1048576], P('interval', None, 'rows')
- ritz_matrix: float32 [4, 64, 64], P('interval')
- ritz_residual: float32 [4, 64, 1048576], P('interval', None, 'rows')
Inputs may be any that keep to these rules, and one draw needn't show every extreme that they name: `filtered`: the rows of each interval's block are linearly independent, and each interval's block shares a part with the block of the interval before it.
All inputs are finite; a program needn't handle non-finite values.
Results may differ from a plain program's by a relative error of at most 0.0003.
Values sent between devices are 32-bit elements; how exact they have to be, the bound alone decides.
A program may use at most 64 MiB of HBM per device.

v0:
```python
import jax
import jax.numpy as jnp
from jax import lax
from jax.sharding import PartitionSpec as P


def from_everyone(x, axis):
    length = lax.axis_size(axis)
    return lax.all_to_all(jnp.broadcast_to(x[None], (length, *x.shape)), axis, 0, 0, tiled=True)


def taken_together(x, axis):
    return from_everyone(x, axis).sum(axis=0)


def from_behind(block, axis, distance):
    devices = range(lax.axis_size(axis))
    route = [(i - distance, i) for i in devices if i - distance in devices]
    return lax.ppermute(block, axis, route)


def with_halo(x, sides, width):
    for axis, dim in sides:
        size, length = (lax.axis_size(axis), x.shape[dim])
        up = [(i, (i + 1) % size) for i in range(size - 1)]
        down = [(j, i) for i, j in up]
        last = lax.slice_in_dim(x, length - width, length, axis=dim)
        leading = lax.slice_in_dim(x, 0, width, axis=dim)
        before = lax.ppermute(last, axis, up)
        after = lax.ppermute(leading, axis, down)
        x = jnp.concatenate([before, x, after], axis=dim)
    return x


def inner(left, right):
    return lax.dot_general(
        left,
        right,
        (((1,), (1,)), ((), ())),
        precision=lax.Precision.HIGHEST,
        preferred_element_type=jnp.float32,
    )


def apply_left(matrix, vectors):
    return jnp.dot(
        matrix, vectors, precision=lax.Precision.HIGHEST, preferred_element_type=jnp.float32
    )


def solve_lower(gram, vectors):
    lower = jnp.linalg.cholesky(gram)
    return lax.linalg.triangular_solve(lower, vectors, left_side=True, lower=True)


def body(filtered, potential):
    vectors = filtered[0]
    width = vectors.shape[0]
    planes_dev = potential.shape[0]
    gram = taken_together(inner(vectors, vectors), "rows")
    own = solve_lower(gram, vectors)
    prior = from_behind(own, "interval", 1)
    cross = taken_together(inner(own, prior), "rows")
    reduced = own - apply_left(cross, prior)
    second = taken_together(inner(reduced, reduced), "rows")
    basis = solve_lower(second, reduced)
    field = basis.reshape(width, planes_dev, potential.shape[1], potential.shape[2])
    padded = with_halo(field, (("rows", 1),), 1)
    beside = padded[:, 2:] + padded[:, :-2]
    framed = jnp.pad(field, ((0, 0), (0, 0), (1, 1), (1, 1)))
    beside = beside + framed[:, :, 2:, 1:-1] + framed[:, :, :-2, 1:-1]
    beside = beside + framed[:, :, 1:-1, 2:] + framed[:, :, 1:-1, :-2]
    image = ((6.0 + potential) * field - beside).reshape(width, -1)
    ritz_matrix = taken_together(inner(basis, image), "rows")
    residual = image - apply_left(ritz_matrix.T, basis)
    return (basis[None], ritz_matrix[None], residual[None])


def solution(mesh):
    return jax.shard_map(
        body,
        mesh=mesh,
        in_specs=(P("interval", None, "rows"), P("rows", None, None)),
        out_specs=(
            P("interval", None, "rows"),
            P("interval", None, None),
            P("interval", None, "rows"),
        ),
        check_vma=False,
    )
```

profile of v0, /device:TPU:1, one launch (start us, length us, event | category | flops | bytes accessed | tf_op | source)
XLA Modules:
  0.0 370.5 jit_solution(10789853556008402481)
XLA Ops:
  0.6 6.9 %fusion.11 = f32[64,64]{1,0:T(8,128)S(1)} fusion(f32[1,64,16384]{2,1,0:T(8,128)} %param.5), kind=kOutput, calls=%fused_computation.19 | convolution fusion | flops 805306368 | bytes 4210688 | tf_op jit(solution)/shard_map/dot_general | solution.py:36
  7.6 0.2 broadcast_in_dim.15
  7.8 1.3 reshape.36
  9.1 41.5 %all_to_all.20 = f32[64,1,4096]{2,1,0:T(1,128)S(1)} all-to-all(f32[64,1,4096]{2,1,0:T(1,128)S(1)} %reshape.36), channel_id=1, replica_groups=mesh['interval'=4,'rows'=64] {'rows'}, dimensions={0} | all-to-all | bytes 2097152 | tf_op jit(solution)/shard_map/all_to_all | solution.py:9
  50.6 0.5 broadcast.42
  51.1 3.3 reduce.4
  54.4 0.8 reshape.37
  55.2 0.2 reduce_sum.36
  55.5 5.8 %cholesky.44 = f32[64,64]{1,0:T(8,128)S(1)} custom-call(f32[64,64]{1,0:T(8,128)S(1)} %fusion.20), custom_call_target="Cholesky" | custom-call | tf_op jit(solution)/shard_map/jit(cholesky)/cholesky | solution.py:52
  61.4 0.6 compare_reduce_fusion.1
  62.0 0.7 fusion.14
  62.7 4.9 %custom-call.6 = f32[1,64,64]{1,2,0:T(8,128)S(1)} custom-call(f32[1,64,64]{2,1,0:T(8,128)S(1)} %fusion.14), custom_call_target="InvertDiagBlocksLowerTriangular" | custom-call | tf_op jit(solution)/shard_map/triangular_solve/custom-call.0 | solution.py:53
  67.6 5.4 %fusion.9 = f32[64,16384]{1,0:T(8,128)S(1)} fusion(f32[1,64,16384]{2,1,0:T(8,128)} %param.5, f32[1,64,64]{1,2,0:T(8,128)S(1)} %custom-call.6), kind=kOutput, calls=%fused_computation.17 | convolution fusion | flops 805306368 | bytes 8404992 | tf_op jit(solution)/shard_map/triangular_solve/dot.1 | solution.py:53
  73.0 8.1 %collective-permute-start = (f32[64,16384]{1,0:T(8,128)S(1)}, f32[64,16384]{1,0:T(8,128)S(1)}, u32[]{:S(2)}, u32[]{:S(2)}) collective-permute-start(f32[64,16384]{1,0:T(8,128)S(1)} %fusion.9), channel_id=1, source_target_pairs={{0,64},{64,128},{128,192},{1,65},{65,129},{129,193},{2,66},{66,130... | collective-permute-start | bytes 12582920 | tf_op jit(solution)/shard_map/ppermute | solution.py:19
  81.1 56.4 %collective-permute-done = f32[64,16384]{1,0:T(8,128)S(1)} collective-permute-done((f32[64,16384]{1,0:T(8,128)S(1)}, f32[64,16384]{1,0:T(8,128)S(1)}, u32[]{:S(2)}, u32[]{:S(2)}) %collective-permute-start) | collective-permute-done | bytes 4194336 | tf_op jit(solution)/shard_map/ppermute | solution.py:19
  137.5 3.5 fusion.24
  141.0 0.2 broadcast_in_dim.16
  141.3 1.3 reshape.38
  142.6 30.5 %all_to_all.21 = f32[64,1,4096]{2,1,0:T(1,128)S(1)} all-to-all(f32[64,1,4096]{2,1,0:T(1,128)S(1)} %reshape.38), channel_id=1, replica_groups=mesh['interval'=4,'rows'=64] {'rows'}, dimensions={0} | all-to-all | bytes 2097152 | tf_op jit(solution)/shard_map/all_to_all | solution.py:9
  173.1 3.3 reduce.5
  176.4 0.8 reshape.39
  177.2 0.2 reduce_sum.37
  177.4 7.2 %convolution_subtract_fusion.1 = f32[64,16384]{1,0:T(8,128)S(1)} fusion(f32[64,16384]{1,0:T(8,128)} %copy-done.3, f32[64,64]{1,0:T(8,128)S(1)} %reduce_sum.37, f32[64,16384]{1,0:T(8,128)} %copy-done.4), kind=kOutput, calls=%fused_computation.1 | convolution fusion | flops 806354944 | bytes 12599296 | tf_op jit(solution)/shard_map/dot_general | solution.py:46
  184.6 3.4 fusion.25
  188.0 0.2 broadcast_in_dim.17
  188.3 1.5 reshape.40
  189.7 24.6 %all_to_all.22 = f32[64,1,4096]{2,1,0:T(1,128)S(1)} all-to-all(f32[64,1,4096]{2,1,0:T(1,128)S(1)} %reshape.40), channel_id=1, replica_groups=mesh['interval'=4,'rows'=64] {'rows'}, dimensions={0} | all-to-all | bytes 2097152 | tf_op jit(solution)/shard_map/all_to_all | solution.py:9
  214.4 3.3 reduce.6
  217.6 0.8 reshape.41
  218.7 5.8 %cholesky.55 = f32[64,64]{1,0:T(8,128)S(1)} custom-call(f32[64,64]{1,0:T(8,128)S(1)} %fusion.18), custom_call_target="Cholesky" | custom-call | tf_op jit(solution)/shard_map/jit(cholesky)/cholesky | solution.py:52
  224.6 0.6 compare_reduce_fusion
  225.3 0.7 fusion.15
  225.9 4.9 %custom-call.7 = f32[1,64,64]{1,2,0:T(8,128)S(1)} custom-call(f32[1,64,64]{2,1,0:T(8,128)S(1)} %fusion.15), custom_call_target="InvertDiagBlocksLowerTriangular" | custom-call | tf_op jit(solution)/shard_map/triangular_solve/custom-call.0 | solution.py:53
  230.8 5.4 %fusion.16 = f32[64,16384]{1,0:T(8,128)S(1)} fusion(f32[64,16384]{1,0:T(8,128)} %copy-done.1, f32[1,64,64]{1,2,0:T(8,128)S(1)} %custom-call.7), kind=kOutput, calls=%fused_computation.26 | convolution fusion | flops 805306368 | bytes 8404992 | tf_op jit(solution)/shard_map/triangular_solve/dot.1 | solution.py:53
  236.3 0.7 copy.9
  237.0 0.6 fusion.23
  237.6 1.3 collective-permute-start.1
  238.9 4.8 %collective-permute-start.2 = (f32[64,1,64,128]{3,2,1,0:T(8,128)S(1)}, f32[64,1,64,128]{3,2,1,0:T(8,128)S(1)}, u32[]{:S(2)}, u32[]{:S(2)}) collective-permute-start(f32[64,1,64,128]{3,2,1,0:T(8,128)S(1)} %get-tuple-element.6), channel_id=1, source_target_pairs={{0,1},{1,2},{2,3},{3,4},{4,5},{5,6},{6,7},{7,8},{8,9},{9,10},{10,1... | collective-permute-start | bytes 6291464 | tf_op jit(solution)/shard_map/ppermute | solution.py:29
  243.8 21.3 %collective-permute-done.1 = f32[64,1,64,128]{3,2,1,0:T(8,128)S(1)} collective-permute-done((f32[64,1,64,128]{3,2,1,0:T(8,128)S(1)}, f32[64,1,64,128]{3,2,1,0:T(8,128)S(1)}, u32[]{:S(2)}, u32[]{:S(2)}) %collective-permute-start.1) | collective-permute-done | bytes 2097184 | tf_op jit(solution)/shard_map/ppermute | solution.py:30
  265.1 4.1 %collective-permute-done.2 = f32[64,1,64,128]{3,2,1,0:T(8,128)S(1)} collective-permute-done((f32[64,1,64,128]{3,2,1,0:T(8,128)S(1)}, f32[64,1,64,128]{3,2,1,0:T(8,128)S(1)}, u32[]{:S(2)}, u32[]{:S(2)}) %collective-permute-start.2) | collective-permute-done | bytes 2097184 | tf_op jit(solution)/shard_map/ppermute | solution.py:29
  269.2 3.6 fusion.5
  272.9 5.6 %fusion.6 = f32[64,64]{1,0:T(8,128)S(1)} fusion(f32[64,16384]{1,0:T(8,128)S(1)} %fusion.16, f32[8,8,128,128]{3,2,1,0:T(8,128)S(1)} %bitcast.48), kind=kOutput, calls=%fused_computation.12 | convolution fusion | flops 805306368 | bytes 8404992 | tf_op jit(solution)/shard_map/dot_general | solution.py:36
  278.5 0.2 broadcast_in_dim.19
  278.8 1.3 reshape.42
  280.1 74.4 %all_to_all.23 = f32[64,1,4096]{2,1,0:T(1,128)S(1)} all-to-all(f32[64,1,4096]{2,1,0:T(1,128)S(1)} %reshape.42), channel_id=1, replica_groups=mesh['interval'=4,'rows'=64] {'rows'}, dimensions={0} | all-to-all | bytes 2097152 | tf_op jit(solution)/shard_map/all_to_all | solution.py:9
  354.5 3.3 reduce.7
  357.7 0.8 reshape.43
  358.8 11.3 %fusion = f32[1,64,16384]{2,1,0:T(8,128)} fusion(f32[64,64]{1,0:T(8,128)S(1)} %reduce_sum.39, f32[64,16384]{1,0:T(8,128)} %copy-done, f32[8,8,128,128]{3,2,1,0:T(8,128)} %bitcast.49), kind=kOutput, calls=%fused_computation.2 | convolution fusion | flops 806354944 | bytes 12599296 | tf_op jit(solution)/shard_map/dot_general | solution.py:46
  (23 shorter events, 0.6 us)
Async XLA Ops:
  73.0 68.0 %copy-start.3 = (f32[64,16384]{1,0:T(8,128)}, f32[64,16384]{1,0:T(8,128)S(1)}, u32[]{:S(2)}) copy-start(f32[64,16384]{1,0:T(8,128)S(1)} %fusion.9) | copy-start | bytes 12582916
  73.0 64.5 %collective-permute-start = (f32[64,16384]{1,0:T(8,128)S(1)}, f32[64,16384]{1,0:T(8,128)S(1)}, u32[]{:S(2)}, u32[]{:S(2)}) collective-permute-start(f32[64,16384]{1,0:T(8,128)S(1)} %fusion.9), channel_id=1, source_target_pairs={{0,64},{64,128},{128,192},{1,65},{65,129},{129,193},{2,66},{66,130... | collective-permute-start | bytes 12582920 | tf_op jit(solution)/shard_map/ppermute | solution.py:19
  137.5 3.5 copy-start.4
  184.6 3.4 copy-start.1
  236.3 36.6 %copy-start = (f32[64,16384]{1,0:T(8,128)}, f32[64,16384]{1,0:T(8,128)S(1)}, u32[]{:S(2)}) copy-start(f32[64,16384]{1,0:T(8,128)S(1)} %fusion.16) | copy-start | bytes 12582916
  237.0 6.7 %copy-start.6 = (f32[2,64,128]{2,1,0:T(8,128)S(1)}, f32[2,64,128]{2,1,0:T(8,128)}, u32[]{:S(2)}) copy-start(f32[2,64,128]{2,1,0:T(8,128)} %param.6) | copy-start | bytes 196612
  237.6 27.5 %collective-permute-start.1 = (f32[64,1,64,128]{3,2,1,0:T(8,128)S(1)}, f32[64,1,64,128]{3,2,1,0:T(8,128)S(1)}, u32[]{:S(2)}, u32[]{:S(2)}) collective-permute-start(f32[64,1,64,128]{3,2,1,0:T(8,128)S(1)} %get-tuple-element.5), channel_id=1, source_target_pairs={{1,0},{2,1},{3,2},{4,3},{5,4},{6,5},{7,6},{8,7},{9,8},{10,9},{11,1... | collective-permute-start | bytes 6291464 | tf_op jit(solution)/shard_map/ppermute | solution.py:30
  238.9 30.3 %collective-permute-start.2 = (f32[64,1,64,128]{3,2,1,0:T(8,128)S(1)}, f32[64,1,64,128]{3,2,1,0:T(8,128)S(1)}, u32[]{:S(2)}, u32[]{:S(2)}) collective-permute-start(f32[64,1,64,128]{3,2,1,0:T(8,128)S(1)} %get-tuple-element.6), channel_id=1, source_target_pairs={{0,1},{1,2},{2,3},{3,4},{4,5},{5,6},{6,7},{7,8},{8,9},{9,10},{10,1... | collective-permute-start | bytes 6291464 | tf_op jit(solution)/shard_map/ppermute | solution.py:29
  272.9 5.7 %copy-start.2 = (f32[64,2,64,128]{3,2,1,0:T(8,128)}, f32[64,2,64,128]{3,2,1,0:T(8,128)S(1)}, u32[]{:S(2)}) copy-start(f32[64,2,64,128]{3,2,1,0:T(8,128)S(1)} %fusion.5) | copy-start | bytes 12582916
  358.7 11.3 %copy-start.5 = (f32[64,64]{1,0:T(8,128)}, f32[64,64]{1,0:T(8,128)S(1)}, u32[]{:S(2)}) copy-start(f32[64,64]{1,0:T(8,128)S(1)} %reduce_sum.39) | copy-start | bytes 49156
where the time goes:
time: 375 us; the launch traced here: 371 us
  blocking collectives  171 us (46%)
  waiting for transfers between devices  81.8 us (22%)
  matrix products  48.8 us (13%)
  other arithmetic  41.6 us (11%)
  starting transfers between devices  14.2 us (4%)
  local copies, waits for them, and re-layouts  11.7 us (3%)
    all_to_all x4, blocking collectives, from_everyone(): lax.all_to_all(jnp.broadcast_to(x[None], (length, *x.shape)), axis, 0, 0,...  171 us
    ppermute x1, waiting for transfers between devices, from_behind(): return lax.ppermute(block, axis, route)  56.4 us
    ppermute x1, waiting for transfers between devices, with_halo(): after = lax.ppermute(leading, axis, down)  21.3 us
    dot_general x4, matrix products, inner(): lax.dot_general(left, right, (((1,), (1,)), ((), ())), precision=lax.Prec...  19.4 us
    dot_general x2, matrix products, apply_left(): jnp.dot(matrix, vectors, precision=lax.Precision.HIGHEST, preferred_eleme...  18.5 us
    all_to_all x4, other arithmetic, from_everyone(): lax.all_to_all(jnp.broadcast_to(x[None], (length, *x.shape)), axis, 0, 0,...  13 us
    another operation x6, other arithmetic, solve_lower(): lower = jnp.linalg.cholesky(gram)  13 us
    another operation x4, other arithmetic, solve_lower(): lax.linalg.triangular_solve(lower, vectors, left_side=True, lower=True)  11.1 us
  transfers between devices with their start and end apart: 3, of which 3 were waited for; matrix products, arithmetic and copies ran while one was open for 0% of the time, Pallas kernels for 0%

commit v1 on v0

v1 whole, which is shorter than its diff:
```python
import jax
import jax.numpy as jnp
from jax import lax
from jax.experimental import pallas as pl
from jax.experimental.pallas import tpu as pltpu
from jax.sharding import PartitionSpec as P

MESH = pl.DeviceIdType.MESH
F32 = jnp.float32
BF16 = jnp.bfloat16

LANES = 128
LAYER = 16
CHUNKS = 8
RELAYS = (3, 7, 11, 4, 8, 12, 6, 9)


def split(v):
    hi = v.astype(BF16)
    return hi, (v - hi.astype(F32)).astype(BF16)


def exact_dot(a, b, dims):
    return lax.dot_general(
        a, b, (dims, ((), ())), precision=lax.Precision.HIGHEST, preferred_element_type=F32
    )


def stencil(u, low, high, pot, plane, j, size, width):
    base = plane * size
    start = pl.multiple_of(base + j * width, LANES)
    c = u[:, pl.ds(start, width)]
    first = pl.multiple_of(jnp.maximum(start - LANES, base), LANES)
    last = pl.multiple_of(jnp.minimum(start + width, base + size - LANES), LANES)
    before = jnp.where(j > 0, u[:, pl.ds(first, LANES)], 0.0)
    after = jnp.where(j < size // width - 1, u[:, pl.ds(last, LANES)], 0.0)
    tiles = width // LANES
    part = [c[:, t * LANES : (t + 1) * LANES] for t in range(tiles)]
    around = [before, *part, after]
    lane = lax.broadcasted_iota(jnp.int32, part[0].shape, 1)
    other = u[:, pl.ds(pl.multiple_of((1 - plane) * size + j * width, LANES), width)]
    halo = (high if plane else low)[:, pl.ds(pl.multiple_of(j * width, LANES), width)]
    weight = 6.0 + pot[:, pl.ds(start, width)]
    out = []
    for t in range(tiles):
        cut = slice(t * LANES, (t + 1) * LANES)
        left = jnp.where(lane == 0, 0.0, pltpu.roll(part[t], 1, 1))
        right = jnp.where(lane == LANES - 1, 0.0, pltpu.roll(part[t], LANES - 1, 1))
        beside = (other[:, cut] + halo[:, cut]) + (around[t] + around[t + 2]) + (left + right)
        out.append(weight[:, cut] * part[t] - beside)
    return jnp.concatenate(out, axis=1)


def inverse_factor(square):
    n = square.shape[0]
    row = lax.broadcasted_iota(jnp.int32, (n, LANES), 0)
    lane = lax.broadcasted_iota(jnp.int32, (n, LANES), 1)
    t = jnp.where(lane < n, square, jnp.where(lane == row + n, 1.0, 0.0))
    for k in range(n):
        pivot = t[k : k + 1, :]
        scaled = pivot * (1.0 / t[k : k + 1, k : k + 1])
        column = jnp.where(row > k, jnp.broadcast_to(t[:, k : k + 1], (n, LANES)), 0.0)
        t = t - column * scaled
    diagonal = jnp.sum(jnp.where(lane == row, t, 0.0), axis=1, keepdims=True)
    t = t * (1.0 / jnp.sqrt(diagonal))
    return pltpu.roll(t, LANES - n, 1)[:, :n]


def coefficients(total, prior, w_out, r_out):
    n = total.shape[0] // 2
    swapped = pltpu.roll(total, n, 1)
    gram, k_own = total[:n, :n], swapped[:n, :n]
    g_pi, k_pi = total[n:, :n], swapped[n:, :n]
    k_prior = pltpu.roll(prior, n, 1)[:, :n]
    inv_p = inverse_factor(prior)
    et = exact_dot(inv_p, g_pi, ((1,), (0,)))
    schur = gram - exact_dot(et, et, ((0,), (0,)))
    wide = jnp.concatenate([schur, jnp.zeros_like(schur)], axis=1)
    a = inverse_factor(wide)
    b = -exact_dot(a, exact_dot(et, inv_p, ((0,), (0,))), ((1,), (0,)))
    mixed = exact_dot(exact_dot(b, k_pi, ((1,), (0,))), a, ((1,), (1,)))
    mixed_t = exact_dot(a, exact_dot(b, k_pi, ((1,), (0,))), ((1,), (1,)))
    ritz = exact_dot(exact_dot(a, k_own, ((1,), (0,))), a, ((1,), (1,)))
    ritz = ritz + mixed + mixed_t
    ritz = ritz + exact_dot(exact_dot(b, k_prior, ((1,), (0,))), b, ((1,), (1,)))
    r_out[...] = ritz
    ra = exact_dot(ritz, a, ((0,), (0,)))
    rb = exact_dot(ritz, b, ((0,), (0,)))
    zero = jnp.zeros_like(a)
    w_out[:n, :] = jnp.concatenate([a, b, zero, zero], axis=1)
    w_out[n:, :] = jnp.concatenate([-ra, -rb, a, b], axis=1)


def exchange_kernel(
    intervals, rows,
    x, pot,
    prev_o, low_o, high_o, plow_o, phigh_o, w_o, r_o,
    prev, low, high, up_a, up_b, down_a, down_b, acc, sums, total, prior,
    x_send, x_recv, up_send, down_send, low_recv, high_recv,
    relay_send, relay_recv, plow_send, phigh_send, plow_recv, phigh_recv,
    out_sem, sum_send, sum_recv, prior_send, prior_recv,
):
    i, r = lax.axis_index("interval"), lax.axis_index("rows")
    layers = rows // LAYER
    layer, q = r // LAYER, r % LAYER
    qx, qy = q // 4, q % 4
    size = low.shape[1]
    width = size // CHUNKS

    def at(c):
        return pl.ds(pl.multiple_of(c * width, LANES), width)

    def remote(src, dst, send, recv, to_i, to_r):
        return pltpu.make_async_remote_copy(
            src_ref=src, dst_ref=dst, send_sem=send, recv_sem=recv,
            device_id=(to_i, to_r), device_id_type=MESH,
        )

    barrier = pltpu.get_barrier_semaphore()

    def greet(to_i, to_r):
        pl.semaphore_signal(barrier, inc=1, device_id=(to_i, to_r), device_id_type=MESH)

    for d in range(1, layers):
        greet(i, lax.rem(layer + d, layers) * LAYER + q)
    for d in range(1, LAYER):
        greet(i, layer * LAYER + lax.rem(q + d, LAYER))
    has_prev, has_next = i > 0, i < intervals - 1
    has_low, has_high = r > 0, r < rows - 1
    for there, to_i, to_r in (
        (has_prev, i - 1, r), (has_next, i + 1, r), (has_low, i, r - 1), (has_high, i, r + 1)
    ):
        pl.when(there)(lambda to_i=to_i, to_r=to_r: greet(to_i, to_r))
    neighbours = (
        has_prev.astype(jnp.int32) + has_next.astype(jnp.int32)
        + has_low.astype(jnp.int32) + has_high.astype(jnp.int32)
    )
    pl.semaphore_wait(barrier, layers - 1 + LAYER - 1 + neighbours)

    last_of_layer, first_of_layer = q == LAYER - 1, q == 0
    cross_up = jnp.logical_and(last_of_layer, has_high)
    cross_down = jnp.logical_and(first_of_layer, has_low)
    plain_up = jnp.logical_not(last_of_layer)
    plain_down = jnp.logical_not(first_of_layer)
    spare = relay_send.at[0]

    def up_plain(c):
        return remote(x.at[:, at(CHUNKS + c)], low.at[:, at(c)], up_send.at[c], low_recv.at[c], i, r + 1)

    def down_plain(c):
        return remote(x.at[:, at(c)], high.at[:, at(c)], down_send.at[c], high_recv.at[c], i, r - 1)

    def up_cross(c):
        return remote(
            x.at[:, at(CHUNKS + c)], up_a, up_send.at[c], relay_recv.at[0], i, layer * LAYER + RELAYS[c]
        )

    def down_cross(c):
        return remote(
            x.at[:, at(c)], down_a, down_send.at[c], relay_recv.at[2], i, layer * LAYER + RELAYS[c]
        )

    def onward(c):
        return remote(x.at[:, at(c)], prev.at[:, at(c)], x_send.at[c], x_recv.at[c], i + 1, r)

    @pl.when(cross_up)
    def _():
        for c in range(CHUNKS):
            up_cross(c).start()

    @pl.when(cross_down)
    def _():
        for c in range(CHUNKS):
            down_cross(c).start()

    def start_onward(first, last):
        @pl.when(has_next)
        def _():
            for c in range(first, last):
                onward(c).start()
                onward(CHUNKS + c).start()

    start_onward(0, CHUNKS // 2)

    @pl.when(plain_up)
    def _():
        for c in range(CHUNKS):
            up_plain(c).start()

    @pl.when(plain_down)
    def _():
        for c in range(CHUNKS):
            down_plain(c).start()

    acc[...] = jnp.zeros_like(acc)

    @pl.when(jnp.logical_not(has_prev))
    def _():
        prev[...] = jnp.zeros_like(prev)

    @pl.when(jnp.logical_not(has_low))
    def _():
        low[...] = jnp.zeros_like(low)

    @pl.when(jnp.logical_not(has_high))
    def _():
        high[...] = jnp.zeros_like(high)

    piece = jnp.int32(0)
    relays = q == RELAYS[0]
    for c in range(1, CHUNKS):
        piece = piece + jnp.where(q == RELAYS[c], c, 0)
        relays = jnp.logical_or(relays, q == RELAYS[c])
    above, below = layer < layers - 1, layer > 0

    def relay_steps():
        base = layer * LAYER
        return (
            (above, 0, up_a, remote(up_a, up_b, relay_send.at[0], relay_recv.at[1], i, r + LAYER)),
            (below, 2, down_a, remote(down_a, down_b, relay_send.at[2], relay_recv.at[3], i, r - LAYER)),
            (below, 1, up_b, remote(
                up_b, low.at[:, at(piece)], relay_send.at[1], low_recv.at[piece], i, base)),
            (above, 3, down_b, remote(
                down_b, high.at[:, at(piece)], relay_send.at[3], high_recv.at[piece], i, base + LAYER - 1)),
        )

    for there, slot, buffer, copy in relay_steps():
        @pl.when(jnp.logical_and(relays, there))
        def _(slot=slot, buffer=buffer, copy=copy):
            remote(buffer, buffer, spare, relay_recv.at[slot], i, r).wait_recv()
            copy.start()

    start_onward(CHUNKS // 2, CHUNKS)

    gives = lax.rem(i, 2) == 0

    def give_low(c):
        return remote(low.at[:, at(c)], plow_o.at[:, at(c)], plow_send.at[c], plow_recv.at[c], i + 1, r)

    def give_high(c):
        return remote(high.at[:, at(c)], phigh_o.at[:, at(c)], phigh_send.at[c], phigh_recv.at[c], i + 1, r)

    def writes(c):
        return (
            pltpu.make_async_copy(prev.at[:, at(c)], prev_o.at[:, at(c)], out_sem.at[0, c]),
            pltpu.make_async_copy(
                prev.at[:, at(CHUNKS + c)], prev_o.at[:, at(CHUNKS + c)], out_sem.at[1, c]),
            pltpu.make_async_copy(low.at[:, at(c)], low_o.at[:, at(c)], out_sem.at[2, c]),
            pltpu.make_async_copy(high.at[:, at(c)], high_o.at[:, at(c)], out_sem.at[3, c]),
        )

    @pl.loop(0, CHUNKS)
    def _(c):
        @pl.when(has_prev)
        def _():
            onward(c).wait_recv()
            onward(CHUNKS + c).wait_recv()

        @pl.when(has_low)
        def _():
            up_plain(c).wait_recv()

        @pl.when(has_high)
        def _():
            down_plain(c).wait_recv()

        for copy in writes(c):
            copy.start()

        @pl.when(gives)
        def _():
            give_low(c).start()
            give_high(c).start()

        for plane in range(2):
            mine = x[:, at(plane * CHUNKS + c)]
            image = stencil(x, low, high, pot, plane, c, size, width)
            theirs = prev[:, at(plane * CHUNKS + c)]
            mine_hi, mine_lo = split(mine)
            image_hi, image_lo = split(image)
            theirs_hi, theirs_lo = split(theirs)
            left = jnp.concatenate([mine_hi, theirs_hi, mine_lo, theirs_lo], axis=0)
            right = jnp.concatenate([mine_hi, image_hi, mine_lo, image_lo], axis=0)
            acc[...] += lax.dot_general(
                left, right, (((1,), (1,)), ((), ())), preferred_element_type=F32
            )

    half = acc.shape[0] // 2
    partial = acc[:half, :half] + acc[half:, half:] + (acc[:half, half:] + acc[half:, :half])

    def summed(stage, mine, place, value):
        sums[stage, mine] = value

        def copy(d):
            return remote(
                sums.at[stage, mine], sums.at[stage, mine],
                sum_send.at[stage, d], sum_recv.at[stage, mine], i, place(lax.rem(mine + d, 4)),
            )

        for d in range(1, 4):
            copy(d).start()
        for d in range(1, 4):
            theirs = lax.rem(mine + d, 4)
            remote(
                sums.at[stage, theirs], sums.at[stage, theirs],
                sum_send.at[stage, d], sum_recv.at[stage, theirs], i, r,
            ).wait_recv()
        return (sums[stage, 0] + sums[stage, 1]) + (sums[stage, 2] + sums[stage, 3])

    partial = summed(0, qy, lambda o: r - qy + o, partial)

    lone = jnp.logical_and(i > 0, lax.rem(i, 2) == 0)

    def pass_up(c):
        return remote(
            prev.at[:, at(CHUNKS + c)], plow_o.at[:, at(c)], up_send.at[c], plow_recv.at[c], i, r + 1)

    def pass_down(c):
        return remote(prev.at[:, at(c)], phigh_o.at[:, at(c)], down_send.at[c], phigh_recv.at[c], i, r - 1)

    def own_low(c):
        return pltpu.make_async_copy(low.at[:, at(c)], plow_o.at[:, at(c)], plow_recv.at[c])

    def own_high(c):
        return pltpu.make_async_copy(high.at[:, at(c)], phigh_o.at[:, at(c)], phigh_recv.at[c])

    def none_low(c):
        return pltpu.make_async_copy(prev.at[:, at(c)], plow_o.at[:, at(c)], plow_recv.at[c])

    def none_high(c):
        return pltpu.make_async_copy(prev.at[:, at(c)], phigh_o.at[:, at(c)], phigh_recv.at[c])

    @pl.when(has_high)
    def _():
        for c in range(CHUNKS):
            up_plain(c).wait_send()

    @pl.when(has_low)
    def _():
        for c in range(CHUNKS):
            down_plain(c).wait_send()

    def for_chunks(there, copies):
        @pl.when(there)
        def _():
            for c in range(CHUNKS):
                for copy in copies:
                    copy(c).start()

    for_chunks(jnp.logical_and(lone, has_high), (pass_up,))
    for_chunks(jnp.logical_and(lone, has_low), (pass_down,))
    for_chunks(jnp.logical_and(lone, jnp.logical_not(has_low)), (own_low,))
    for_chunks(jnp.logical_and(lone, jnp.logical_not(has_high)), (own_high,))
    for_chunks(jnp.logical_not(has_prev), (none_low, none_high))

    partial = summed(1, qx, lambda o: r - qx * 4 + o * 4, partial)
    partial = summed(2, layer, lambda o: o * LAYER + q, partial)
    total[...] = partial
    n = prior.shape[0]
    hand = remote(total.at[pl.ds(0, n)], prior, prior_send, prior_recv, i + 1, r)
    pl.when(has_next)(lambda: hand.start())
    pl.when(has_prev)(lambda: hand.wait_recv())

    @pl.when(jnp.logical_not(has_prev))
    def _():
        row = lax.broadcasted_iota(jnp.int32, prior.shape, 0)
        lane = lax.broadcasted_iota(jnp.int32, prior.shape, 1)
        prior[...] = jnp.where(row == lane, 1.0, 0.0)

    coefficients(total[...], prior[...], w_o, r_o)

    for c in range(CHUNKS):
        for copy in writes(c):
            copy.wait()
        give_low(c).wait_recv()
        give_high(c).wait_recv()

    @pl.when(has_next)
    def _():
        hand.wait_send()
        for c in range(2 * CHUNKS):
            onward(c).wait_send()

    @pl.when(gives)
    def _():
        for c in range(CHUNKS):
            give_low(c).wait_send()
            give_high(c).wait_send()

    @pl.when(jnp.logical_and(lone, has_high))
    def _():
        for c in range(CHUNKS):
            pass_up(c).wait_send()

    @pl.when(jnp.logical_and(lone, has_low))
    def _():
        for c in range(CHUNKS):
            pass_down(c).wait_send()

    for there, slot, buffer, copy in relay_steps():
        @pl.when(jnp.logical_and(relays, there))
        def _(copy=copy):
            copy.wait_send()

    for stage in range(3):
        for d in range(1, 4):
            remote(
                sums.at[stage, 0], sums.at[stage, 0],
                sum_send.at[stage, d], sum_recv.at[stage, 0], i, r,
            ).wait_send()


def apply_kernel(
    x_h, prev_h, low_h, high_h, plow_h, phigh_h, pot, w, basis_o, residual_o,
    x, prev, low, high, plow, phigh, out, in_sem, out_sem,
):
    size = low.shape[1]
    width = size // CHUNKS
    n = x.shape[0]

    def at(c):
        return pl.ds(pl.multiple_of(c * width, LANES), width)

    def reads(c):
        pairs = (
            (x_h, x, c), (x_h, x, CHUNKS + c), (prev_h, prev, c), (prev_h, prev, CHUNKS + c),
            (low_h, low, c), (high_h, high, c), (plow_h, plow, c), (phigh_h, phigh, c),
        )
        return [
            pltpu.make_async_copy(src.at[:, at(k)], dst.at[:, at(k)], in_sem.at[e, c])
            for e, (src, dst, k) in enumerate(pairs)
        ]

    for c in range(CHUNKS):
        for copy in reads(c):
            copy.start()

    def writes(plane, c):
        where = at(plane * CHUNKS + c)
        return [
            pltpu.make_async_copy(out.at[plane, pl.ds(e * n, n)], dst.at[:, where], out_sem.at[plane, e])
            for e, dst in enumerate((basis_o, residual_o))
        ]

    w_hi, w_lo = split(w[...])
    both = jnp.concatenate([w_hi, w_lo], axis=0)
    for copy in reads(0):
        copy.wait()

    @pl.loop(0, CHUNKS)
    def _(c):
        @pl.when(c < CHUNKS - 1)
        def _():
            for copy in reads(c + 1):
                copy.wait()

        for plane in range(2):
            k = plane * CHUNKS + c
            z = jnp.concatenate(
                [
                    x[:, at(k)],
                    prev[:, at(k)],
                    stencil(x, low, high, pot, plane, c, size, width),
                    stencil(prev, plow, phigh, pot, plane, c, size, width),
                ],
                axis=0,
            )
            z_hi, z_lo = split(z)
            wide = jnp.dot(both, z_hi, preferred_element_type=F32)
            value = (wide[: 2 * n] + wide[2 * n :]) + jnp.dot(w_hi, z_lo, preferred_element_type=F32)

            @pl.when(c > 0)
            def _():
                for copy in writes(plane, c - 1):
                    copy.wait()

            out[plane] = value
            for copy in writes(plane, c):
                copy.start()

    for plane in range(2):
        for copy in writes(plane, CHUNKS - 1):
            copy.wait()


def solution(mesh):
    intervals, rows = mesh.shape["interval"], mesh.shape["rows"]

    def body(filtered, potential):
        x = filtered[0]
        n, cells = x.shape
        size = cells // 2
        width = size // CHUNKS
        pot = potential.reshape(1, cells)
        anywhere = pl.BlockSpec(memory_space=pl.ANY)
        vmem = pl.BlockSpec(memory_space=pltpu.VMEM)
        whole = jax.ShapeDtypeStruct((n, cells), F32)
        plane = jax.ShapeDtypeStruct((n, size), F32)
        dma = pltpu.SemaphoreType.DMA

        def kernel(*refs):
            exchange_kernel(intervals, rows, *refs)

        prev, low, high, plow, phigh, w, ritz = pl.pallas_call(
            kernel,
            out_shape=(
                whole, plane, plane, plane, plane,
                jax.ShapeDtypeStruct((2 * n, 4 * n), F32),
                jax.ShapeDtypeStruct((n, n), F32),
            ),
            in_specs=[vmem, vmem],
            out_specs=(anywhere,) * 5 + (vmem, vmem),
            scratch_shapes=[
                pltpu.VMEM((n, cells), F32),
                pltpu.VMEM((n, size), F32),
                pltpu.VMEM((n, size), F32),
                *[pltpu.VMEM((n, width), F32) for _ in range(4)],
                pltpu.VMEM((4 * n, 4 * n), F32),
                pltpu.VMEM((3, 4, 2 * n, 2 * n), F32),
                pltpu.VMEM((2 * n, 2 * n), F32),
                pltpu.VMEM((n, 2 * n), F32),
                dma((2 * CHUNKS,)), dma((2 * CHUNKS,)),
                dma((CHUNKS,)), dma((CHUNKS,)), dma((CHUNKS,)), dma((CHUNKS,)),
                dma((4,)), dma((4,)),
                dma((CHUNKS,)), dma((CHUNKS,)), dma((CHUNKS,)), dma((CHUNKS,)),
                dma((4, CHUNKS)),
                dma((3, 4)), dma((3, 4)),
                dma, dma,
            ],
            compiler_params=pltpu.CompilerParams(
                collective_id=0, has_side_effects=True, vmem_limit_bytes=48 * 2**20
            ),
            name="exchange",
        )(x, pot)
        basis, residual = pl.pallas_call(
            apply_kernel,
            out_shape=(whole, whole),
            in_specs=[anywhere] * 6 + [vmem, vmem],
            out_specs=(anywhere, anywhere),
            scratch_shapes=[
                pltpu.VMEM((n, cells), F32),
                pltpu.VMEM((n, cells), F32),
                *[pltpu.VMEM((n, size), F32) for _ in range(4)],
                pltpu.VMEM((2, 2 * n, width), F32),
                dma((8, CHUNKS)), dma((2, 2)),
            ],
            compiler_params=pltpu.CompilerParams(vmem_limit_bytes=48 * 2**20),
            name="apply",
        )(x, prev, low, high, plow, phigh, pot, w)
        return basis[None], ritz[None], residual[None]

    return jax.shard_map(
        body,
        mesh=mesh,
        in_specs=(P("interval", None, "rows"), P("rows", None, None)),
        out_specs=(
            P("interval", None, "rows"),
            P("interval", None, None),
            P("interval", None, "rows"),
        ),
        check_vma=False,
    )
```

time: 375 us -> 174 us (0.46)
  the two profiles are of different devices: /device:TPU:1 before, /device:TPU:61 now
where the time goes in v1:
time: 174 us
  Pallas kernels  172 us (99%)
    pallas_call x1, Pallas kernels, body(): pl.pallas_call(kernel, out_shape=(whole, plane, plane, plane, plane, jax....  158 us
    pallas_call x1, Pallas kernels, body(): pl.pallas_call(apply_kernel, out_shape=(whole, whole), in_specs=[anywhere...  14.2 us

profile of v1, /device:TPU:61, one launch (start us, length us, event | category | flops | bytes accessed | tf_op | source)
XLA Modules:
  0.0 174.0 jit_solution(7426358214941970538)
XLA Ops:
  0.6 0.0 copy-start
  0.6 0.8 copy-done
  1.5 157.7 %exchange.1 = (f32[64,16384]{1,0:T(8,128)}, f32[64,8192]{1,0:T(8,128)S(1)}, f32[64,8192]{1,0:T(8,128)S(1)}, f32[64,8192]{1,0:T(8,128)}, f32[64,8192]{1,0:T(8,128...) custom-call(f32[64,16384]{1,0:T(8,128)} %bitcast.8, f32[1,16384]{1,0:T(1,128)S(1)} %bitcast.5), custom_call_target="tpu_custom_call" | custom-call | tf_op jit(solution)/shard_map/exchange/pallas_call | solution.py:504
  159.1 14.2 %apply.1 = (f32[64,16384]{1,0:T(8,128)}, f32[64,16384]{1,0:T(8,128)}) custom-call(f32[64,16384]{1,0:T(8,128)} %bitcast.9, f32[64,16384]{1,0:T(8,128)} %get-tuple-element.12.prev_h, f32[64,8192]{1,0:T(8,128)S(1)} %get-tuple-element.13.low_h, f32[64,8192]{1,0:T(8,128)S(1)} %get-tuple-element.14.high_h, f32[64,8192]{1,0:T(8,128)} %get-tuple-element.15.plow_h, ...), custom_call_target="tpu_custom_call" | custom-call | tf_op jit(solution)/shard_map/apply/pallas_call | solution.py:535
  173.3 0.6 copy.6
Async XLA Ops:
  0.6 0.8 copy-start

commit v2 on v1

--- a/solution.py
+++ b/solution.py
@@ -1,3 +1,5 @@
+import functools
+
 import jax
 import jax.numpy as jnp
 from jax import lax
@@ -12,7 +14,12 @@
 LANES = 128
 LAYER = 16
 CHUNKS = 8
-RELAYS = (3, 7, 11, 4, 8, 12, 6, 9)
+RELAYS = {0: 3, 1: 7, 2: 10, 5: 9, 6: 13, 7: 8}
+OWN, STRAIGHT = 3, 4
+FIRST_CROSS, THEN_CROSS = (6,), (0, 2, 3, 1, 7, 4, 5)
+ACROSS, BESIDE = (2, 5, 7), (0, 1, 3, 4, 6)
+FIRST_ONWARD, NEXT_ONWARD = 2, 4
+INVERT_AT = 4
 
 
 def split(v):
@@ -66,22 +73,22 @@
     return pltpu.roll(t, LANES - n, 1)[:, :n]
 
 
-def coefficients(total, prior, w_out, r_out):
+def coefficients(total, inv_p, prior, wait_prior, w_out, r_out):
     n = total.shape[0] // 2
     swapped = pltpu.roll(total, n, 1)
     gram, k_own = total[:n, :n], swapped[:n, :n]
     g_pi, k_pi = total[n:, :n], swapped[n:, :n]
-    k_prior = pltpu.roll(prior, n, 1)[:, :n]
-    inv_p = inverse_factor(prior)
     et = exact_dot(inv_p, g_pi, ((1,), (0,)))
     schur = gram - exact_dot(et, et, ((0,), (0,)))
+    toward = exact_dot(et, inv_p, ((0,), (0,)))
     wide = jnp.concatenate([schur, jnp.zeros_like(schur)], axis=1)
     a = inverse_factor(wide)
-    b = -exact_dot(a, exact_dot(et, inv_p, ((0,), (0,))), ((1,), (0,)))
-    mixed = exact_dot(exact_dot(b, k_pi, ((1,), (0,))), a, ((1,), (1,)))
-    mixed_t = exact_dot(a, exact_dot(b, k_pi, ((1,), (0,))), ((1,), (1,)))
+    b = -exact_dot(a, toward, ((1,), (0,)))
+    mixed = exact_dot(b, k_pi, ((1,), (0,)))
     ritz = exact_dot(exact_dot(a, k_own, ((1,), (0,))), a, ((1,), (1,)))
-    ritz = ritz + mixed + mixed_t
+    ritz = ritz + exact_dot(mixed, a, ((1,), (1,))) + exact_dot(a, mixed, ((1,), (1,)))
+    wait_prior()
+    k_prior = pltpu.roll(prior[...], n, 1)[:, :n]
     ritz = ritz + exact_dot(exact_dot(b, k_prior, ((1,), (0,))), b, ((1,), (1,)))
     r_out[...] = ritz
     ra = exact_dot(ritz, a, ((0,), (0,)))
@@ -93,12 +100,13 @@
 
 def exchange_kernel(
     intervals, rows,
-    x, pot,
+    x_h, pot,
     prev_o, low_o, high_o, plow_o, phigh_o, w_o, r_o,
-    prev, low, high, up_a, up_b, down_a, down_b, acc, sums, total, prior,
+    x, prev, low, high, up_a, up_b, down_a, down_b, acc, sums, total, prior, early_sums, early_total, early_prior, inv_p,
     x_send, x_recv, up_send, down_send, low_recv, high_recv,
-    relay_send, relay_recv, plow_send, phigh_send, plow_recv, phigh_recv,
-    out_sem, sum_send, sum_recv, prior_send, prior_recv,
+    relay_send, relay_recv, pass_up_send, pass_down_send, plow_send, phigh_send, plow_recv, phigh_recv,
+    in_sem, out_sem, sum_send, sum_recv, prior_send, prior_recv,
+    early_send, early_recv, early_prior_send, early_prior_recv,
 ):
     i, r = lax.axis_index("interval"), lax.axis_index("rows")
     layers = rows // LAYER
@@ -115,6 +123,12 @@
             src_ref=src, dst_ref=dst, send_sem=send, recv_sem=recv,
             device_id=(to_i, to_r), device_id_type=MESH,
         )
+
+    loads = [
+        pltpu.make_async_copy(x_h.at[:, at(c)], x.at[:, at(c)], in_sem.at[c]) for c in range(2 * CHUNKS)
+    ]
+    for copy in loads:
+        copy.start()
 
     barrier = pltpu.get_barrier_semaphore()
 
@@ -135,7 +149,51 @@
         has_prev.astype(jnp.int32) + has_next.astype(jnp.int32)
         + has_low.astype(jnp.int32) + has_high.astype(jnp.int32)
     )
+    for copy in loads:
+        copy.wait()
+    n = prior.shape[0]
+    early_acc = acc.at[pl.ds(0, 2 * n), pl.ds(0, 2 * n)]
+    early_acc[...] = jnp.zeros((2 * n, 2 * n), F32)
+
+    @pl.loop(0, 2 * CHUNKS)
+    def _(c):
+        both = jnp.concatenate(split(x[:, at(c)]), axis=0)
+        early_acc[...] += lax.dot_general(
+            both, both, (((1,), (1,)), ((), ())), preferred_element_type=F32
+        )
+
+    halves = early_acc[pl.ds(0, n), :] + pltpu.roll(early_acc[pl.ds(n, n), :], n, 1)
+    own_gram = halves + pltpu.roll(halves, n, 1)
     pl.semaphore_wait(barrier, layers - 1 + LAYER - 1 + neighbours)
+
+    places = (
+        (qy, lambda o: r - qy + o), (qx, lambda o: r - qx * 4 + o * 4), (layer, lambda o: o * LAYER + q)
+    )
+
+    def sum_copy(buffer, send, recv, stage, slot, d, to_r):
+        return remote(
+            buffer.at[stage, slot], buffer.at[stage, slot], send.at[stage, d], recv.at[stage, slot], i, to_r)
+
+    def sum_start(buffer, send, recv, stage, value):
+        mine, place = places[stage]
+        buffer[stage, mine] = value
+        for d in range(1, 4):
+            sum_copy(buffer, send, recv, stage, mine, d, place(lax.rem(mine + d, 4))).start()
+
+    def sum_end(buffer, send, recv, stage):
+        mine, _ = places[stage]
+        for d in range(1, 4):
+            sum_copy(buffer, send, recv, stage, lax.rem(mine + d, 4), d, r).wait_recv()
+        return (buffer[stage, 0] + buffer[stage, 1]) + (buffer[stage, 2] + buffer[stage, 3])
+
+    early = (early_sums, early_send, early_recv)
+    late = (sums, sum_send, sum_recv)
+
+    def summed(stage, value):
+        sum_start(*late, stage, value)
+        return sum_end(*late, stage)
+
+    sum_start(*early, 0, own_gram)
 
     last_of_layer, first_of_layer = q == LAYER - 1, q == 0
     cross_up = jnp.logical_and(last_of_layer, has_high)
@@ -150,47 +208,56 @@
     def down_plain(c):
         return remote(x.at[:, at(c)], high.at[:, at(c)], down_send.at[c], high_recv.at[c], i, r - 1)
 
+    base = layer * LAYER
+
     def up_cross(c):
-        return remote(
-            x.at[:, at(CHUNKS + c)], up_a, up_send.at[c], relay_recv.at[0], i, layer * LAYER + RELAYS[c]
+        if c == STRAIGHT:
+            return up_plain(c)
+        dst, recv, to = (up_b, 1, r + LAYER) if c == OWN else (up_a, 0, base + RELAYS[c])
+        return remote(x.at[:, at(CHUNKS + c)], dst, up_send.at[c], relay_recv.at[recv], i, to)
+
+    def down_cross(c):
+        if c == STRAIGHT:
+            return down_plain(c)
+        dst, recv, to = (
+            (down_b, 3, r - LAYER) if c == OWN else (down_a, 2, base + LAYER - 1 - RELAYS[c])
         )
-
-    def down_cross(c):
-        return remote(
-            x.at[:, at(c)], down_a, down_send.at[c], relay_recv.at[2], i, layer * LAYER + RELAYS[c]
-        )
+        return remote(x.at[:, at(c)], dst, down_send.at[c], relay_recv.at[recv], i, to)
 
     def onward(c):
         return remote(x.at[:, at(c)], prev.at[:, at(c)], x_send.at[c], x_recv.at[c], i + 1, r)
 
-    @pl.when(cross_up)
-    def _():
-        for c in range(CHUNKS):
-            up_cross(c).start()
-
-    @pl.when(cross_down)
-    def _():
-        for c in range(CHUNKS):
-            down_cross(c).start()
+    def start_chunks(there, copies, chunks):
+        @pl.when(there)
+        def _():
+            for c in chunks:
+                for copy in copies:
+                    copy(c).start()
+
+    def onward_low(c):
+        return onward(c)
+
+    def onward_high(c):
+        return onward(CHUNKS + c)
 
     def start_onward(first, last):
-        @pl.when(has_next)
-        def _():
-            for c in range(first, last):
-                onward(c).start()
-                onward(CHUNKS + c).start()
-
-    start_onward(0, CHUNKS // 2)
-
-    @pl.when(plain_up)
-    def _():
-        for c in range(CHUNKS):
-            up_plain(c).start()
-
-    @pl.when(plain_down)
-    def _():
-        for c in range(CHUNKS):
-            down_plain(c).start()
+        start_chunks(has_next, (onward_low, onward_high), range(first, last))
+
+    all_of = lambda *terms: functools.reduce(jnp.logical_and, terms)
+    start_onward(0, FIRST_ONWARD)
+    start_chunks(cross_up, (up_cross,), FIRST_CROSS)
+    start_chunks(cross_down, (down_cross,), FIRST_CROSS)
+    start_chunks(qy < 3, (up_plain,), range(CHUNKS))
+    start_chunks(qy > 0, (down_plain,), range(CHUNKS))
+    own_gram = sum_end(*early, 0)
+    sum_start(*early, 1, own_gram)
+    start_chunks(cross_up, (up_cross,), THEN_CROSS)
+    start_chunks(cross_down, (down_cross,), THEN_CROSS)
+    start_chunks(all_of(qy == 3, plain_up), (up_plain,), range(CHUNKS))
+    start_chunks(all_of(qy == 0, plain_down), (down_plain,), range(CHUNKS))
+    own_gram = sum_end(*early, 1)
+    sum_start(*early, 2, own_gram)
+    start_onward(FIRST_ONWARD, NEXT_ONWARD)
 
     acc[...] = jnp.zeros_like(acc)
 
@@ -206,33 +273,55 @@
     def _():
         high[...] = jnp.zeros_like(high)
 
-    piece = jnp.int32(0)
-    relays = q == RELAYS[0]
-    for c in range(1, CHUNKS):
-        piece = piece + jnp.where(q == RELAYS[c], c, 0)
-        relays = jnp.logical_or(relays, q == RELAYS[c])
+    def role(column):
+        chunk, first = jnp.int32(0), jnp.bool_(False)
+        for c, of in RELAYS.items():
+            chunk = chunk + jnp.where(column == of, c, 0)
+            first = jnp.logical_or(first, column == of)
+        own = column == LAYER - 1
+        return chunk + jnp.where(own, OWN, 0), first, jnp.logical_or(first, own)
+
+    up_chunk, up_first, up_second = role(q)
+    down_chunk, down_first, down_second = role(LAYER - 1 - q)
     above, below = layer < layers - 1, layer > 0
-
-    def relay_steps():
-        base = layer * LAYER
-        return (
-            (above, 0, up_a, remote(up_a, up_b, relay_send.at[0], relay_recv.at[1], i, r + LAYER)),
-            (below, 2, down_a, remote(down_a, down_b, relay_send.at[2], relay_recv.at[3], i, r - LAYER)),
-            (below, 1, up_b, remote(
-                up_b, low.at[:, at(piece)], relay_send.at[1], low_recv.at[piece], i, base)),
-            (above, 3, down_b, remote(
-                down_b, high.at[:, at(piece)], relay_send.at[3], high_recv.at[piece], i, base + LAYER - 1)),
-        )
-
-    for there, slot, buffer, copy in relay_steps():
-        @pl.when(jnp.logical_and(relays, there))
-        def _(slot=slot, buffer=buffer, copy=copy):
-            remote(buffer, buffer, spare, relay_recv.at[slot], i, r).wait_recv()
-            copy.start()
-
-    start_onward(CHUNKS // 2, CHUNKS)
+    first_hops = (
+        (jnp.logical_and(up_first, above), 0, up_a, remote(
+            up_a, up_b, relay_send.at[0], relay_recv.at[1], i, r + LAYER)),
+        (jnp.logical_and(down_first, below), 2, down_a, remote(
+            down_a, down_b, relay_send.at[2], relay_recv.at[3], i, r - LAYER)),
+    )
+    second_hops = (
+        (jnp.logical_and(up_second, below), 1, up_b, remote(
+            up_b, low.at[:, at(up_chunk)], relay_send.at[1], low_recv.at[up_chunk], i, base)),
+        (jnp.logical_and(down_second, above), 3, down_b, remote(
+            down_b, high.at[:, at(down_chunk)], relay_send.at[3], high_recv.at[down_chunk],
+            i, base + LAYER - 1)),
+    )
+
+    def relay(hops):
+        for there, slot, buffer, copy in hops:
+            @pl.when(there)
+            def _(slot=slot, buffer=buffer, copy=copy):
+                remote(buffer, buffer, spare, relay_recv.at[slot], i, r).wait_recv()
+                copy.start()
+
+    relay(first_hops)
+    start_onward(NEXT_ONWARD, CHUNKS)
+    relay(second_hops)
+    early_total[...] = sum_end(*early, 2)
+    early_hand = remote(early_total, early_prior, early_prior_send, early_prior_recv, i + 1, r)
+    pl.when(has_next)(lambda: early_hand.start())
+
+    @pl.when(jnp.logical_not(has_prev))
+    def _():
+        row = lax.broadcasted_iota(jnp.int32, early_prior.shape, 0)
+        lane = lax.broadcasted_iota(jnp.int32, early_prior.shape, 1)
+        early_prior[...] = jnp.where(row == lane, 1.0, 0.0)
+        prior[...] = jnp.zeros_like(prior)
+
 
     gives = lax.rem(i, 2) == 0
+    across = jnp.logical_and(has_next, jnp.logical_not(gives))
 
     def give_low(c):
         return remote(low.at[:, at(c)], plow_o.at[:, at(c)], plow_send.at[c], plow_recv.at[c], i + 1, r)
@@ -249,8 +338,16 @@
             pltpu.make_async_copy(high.at[:, at(c)], high_o.at[:, at(c)], out_sem.at[3, c]),
         )
 
+    lone = jnp.logical_and(has_prev, gives)
+
+    def invert():
+        pl.when(has_prev)(lambda: early_hand.wait_recv())
+        inv_p[...] = inverse_factor(early_prior[...])
+
     @pl.loop(0, CHUNKS)
     def _(c):
+        pl.when(jnp.logical_and(c == INVERT_AT, jnp.logical_not(lone)))(invert)
+
         @pl.when(has_prev)
         def _():
             onward(c).wait_recv()
@@ -288,35 +385,19 @@
     half = acc.shape[0] // 2
     partial = acc[:half, :half] + acc[half:, half:] + (acc[:half, half:] + acc[half:, :half])
 
-    def summed(stage, mine, place, value):
-        sums[stage, mine] = value
-
-        def copy(d):
-            return remote(
-                sums.at[stage, mine], sums.at[stage, mine],
-                sum_send.at[stage, d], sum_recv.at[stage, mine], i, place(lax.rem(mine + d, 4)),
-            )
-
-        for d in range(1, 4):
-            copy(d).start()
-        for d in range(1, 4):
-            theirs = lax.rem(mine + d, 4)
-            remote(
-                sums.at[stage, theirs], sums.at[stage, theirs],
-                sum_send.at[stage, d], sum_recv.at[stage, theirs], i, r,
-            ).wait_recv()
-        return (sums[stage, 0] + sums[stage, 1]) + (sums[stage, 2] + sums[stage, 3])
-
-    partial = summed(0, qy, lambda o: r - qy + o, partial)
-
-    lone = jnp.logical_and(i > 0, lax.rem(i, 2) == 0)
-
     def pass_up(c):
         return remote(
-            prev.at[:, at(CHUNKS + c)], plow_o.at[:, at(c)], up_send.at[c], plow_recv.at[c], i, r + 1)
+            prev.at[:, at(CHUNKS + c)], plow_o.at[:, at(c)], pass_up_send.at[c], plow_recv.at[c], i, r + 1)
 
     def pass_down(c):
-        return remote(prev.at[:, at(c)], phigh_o.at[:, at(c)], down_send.at[c], phigh_recv.at[c], i, r - 1)
+        return remote(
+            prev.at[:, at(c)], phigh_o.at[:, at(c)], pass_down_send.at[c], phigh_recv.at[c], i, r - 1)
+
+    def none_low(c):
+        return pltpu.make_async_copy(prev.at[:, at(c)], plow_o.at[:, at(c)], plow_recv.at[c])
+
+    def none_high(c):
+        return pltpu.make_async_copy(prev.at[:, at(c)], phigh_o.at[:, at(c)], phigh_recv.at[c])
 
     def own_low(c):
         return pltpu.make_async_copy(low.at[:, at(c)], plow_o.at[:, at(c)], plow_recv.at[c])
@@ -324,50 +405,22 @@
     def own_high(c):
         return pltpu.make_async_copy(high.at[:, at(c)], phigh_o.at[:, at(c)], phigh_recv.at[c])
 
-    def none_low(c):
-        return pltpu.make_async_copy(prev.at[:, at(c)], plow_o.at[:, at(c)], plow_recv.at[c])
-
-    def none_high(c):
-        return pltpu.make_async_copy(prev.at[:, at(c)], phigh_o.at[:, at(c)], phigh_recv.at[c])
-
-    @pl.when(has_high)
-    def _():
-        for c in range(CHUNKS):
-            up_plain(c).wait_send()
-
-    @pl.when(has_low)
-    def _():
-        for c in range(CHUNKS):
-            down_plain(c).wait_send()
-
-    def for_chunks(there, copies):
-        @pl.when(there)
-        def _():
-            for c in range(CHUNKS):
-                for copy in copies:
-                    copy(c).start()
-
-    for_chunks(jnp.logical_and(lone, has_high), (pass_up,))
-    for_chunks(jnp.logical_and(lone, has_low), (pass_down,))
-    for_chunks(jnp.logical_and(lone, jnp.logical_not(has_low)), (own_low,))
-    for_chunks(jnp.logical_and(lone, jnp.logical_not(has_high)), (own_high,))
-    for_chunks(jnp.logical_not(has_prev), (none_low, none_high))
-
-    partial = summed(1, qx, lambda o: r - qx * 4 + o * 4, partial)
-    partial = summed(2, layer, lambda o: o * LAYER + q, partial)
+    start_chunks(jnp.logical_not(has_prev), (none_low, none_high), range(CHUNKS))
+    start_chunks(all_of(lone, jnp.logical_not(has_low)), (own_low,), BESIDE)
+    start_chunks(all_of(lone, jnp.logical_not(has_high)), (own_high,), BESIDE)
+    sum_start(*late, 0, partial)
+    pl.when(lone)(invert)
+    partial = sum_end(*late, 0)
+    partial = summed(1, partial)
+    partial = summed(2, partial)
     total[...] = partial
-    n = prior.shape[0]
     hand = remote(total.at[pl.ds(0, n)], prior, prior_send, prior_recv, i + 1, r)
     pl.when(has_next)(lambda: hand.start())
-    pl.when(has_prev)(lambda: hand.wait_recv())
-
-    @pl.when(jnp.logical_not(has_prev))
-    def _():
-        row = lax.broadcasted_iota(jnp.int32, prior.shape, 0)
-        lane = lax.broadcasted_iota(jnp.int32, prior.shape, 1)
-        prior[...] = jnp.where(row == lane, 1.0, 0.0)
-
-    coefficients(total[...], prior[...], w_o, r_o)
+    start_chunks(all_of(lone, has_high), (pass_up,), BESIDE)
+    start_chunks(all_of(lone, has_low), (pass_down,), BESIDE)
+    start_chunks(across, (give_low, give_high), ACROSS)
+    wait_prior = lambda: pl.when(has_prev)(lambda: hand.wait_recv())
+    coefficients(total[...], inv_p[...], prior, wait_prior, w_o, r_o)
 
     for c in range(CHUNKS):
         for copy in writes(c):
@@ -375,39 +428,29 @@
         give_low(c).wait_recv()
         give_high(c).wait_recv()
 
-    @pl.when(has_next)
-    def _():
-        hand.wait_send()
-        for c in range(2 * CHUNKS):
-            onward(c).wait_send()
-
-    @pl.when(gives)
-    def _():
-        for c in range(CHUNKS):
-            give_low(c).wait_send()
-            give_high(c).wait_send()
-
-    @pl.when(jnp.logical_and(lone, has_high))
-    def _():
-        for c in range(CHUNKS):
-            pass_up(c).wait_send()
-
-    @pl.when(jnp.logical_and(lone, has_low))
-    def _():
-        for c in range(CHUNKS):
-            pass_down(c).wait_send()
-
-    for there, slot, buffer, copy in relay_steps():
-        @pl.when(jnp.logical_and(relays, there))
-        def _(copy=copy):
-            copy.wait_send()
+    def end_chunks(there, copies, chunks):
+        @pl.when(there)
+        def _():
+            for c in chunks:
+                for copy in copies:
+                    copy(c).wait_send()
+
+    end_chunks(has_high, (up_plain,), range(CHUNKS))
+    end_chunks(has_low, (down_plain,), range(CHUNKS))
+    pl.when(has_next)(lambda: hand.wait_send())
+    pl.when(has_next)(lambda: early_hand.wait_send())
+    end_chunks(has_next, (onward,), range(2 * CHUNKS))
+    end_chunks(gives, (give_low, give_high), range(CHUNKS))
+    end_chunks(across, (give_low, give_high), ACROSS)
+    end_chunks(all_of(lone, has_high), (pass_up,), BESIDE)
+    end_chunks(all_of(lone, has_low), (pass_down,), BESIDE)
+    for there, _, _, copy in first_hops + second_hops:
+        pl.when(there)(lambda copy=copy: copy.wait_send())
 
     for stage in range(3):
         for d in range(1, 4):
-            remote(
-                sums.at[stage, 0], sums.at[stage, 0],
-                sum_send.at[stage, d], sum_recv.at[stage, 0], i, r,
-            ).wait_send()
+            sum_copy(*early, stage, 0, d, r).wait_send()
+            sum_copy(*late, stage, 0, d, r).wait_send()
 
 
 def apply_kernel(
@@ -508,9 +551,10 @@
                 jax.ShapeDtypeStruct((2 * n, 4 * n), F32),
                 jax.ShapeDtypeStruct((n, n), F32),
             ),
-            in_specs=[vmem, vmem],
+            in_specs=[anywhere, vmem],
             out_specs=(anywhere,) * 5 + (vmem, vmem),
             scratch_shapes=[
+                pltpu.VMEM((n, cells), F32),
                 pltpu.VMEM((n, cells), F32),
                 pltpu.VMEM((n, size), F32),
                 pltpu.VMEM((n, size), F32),
@@ -519,11 +563,18 @@
                 pltpu.VMEM((3, 4, 2 * n, 2 * n), F32),
                 pltpu.VMEM((2 * n, 2 * n), F32),
                 pltpu.VMEM((n, 2 * n), F32),
+                pltpu.VMEM((3, 4, n, 2 * n), F32),
+                pltpu.VMEM((n, 2 * n), F32),
+                pltpu.VMEM((n, 2 * n), F32),
+                pltpu.VMEM((n, n), F32),
                 dma((2 * CHUNKS,)), dma((2 * CHUNKS,)),
                 dma((CHUNKS,)), dma((CHUNKS,)), dma((CHUNKS,)), dma((CHUNKS,)),
                 dma((4,)), dma((4,)),
+                dma((CHUNKS,)), dma((CHUNKS,)),
                 dma((CHUNKS,)), dma((CHUNKS,)), dma((CHUNKS,)), dma((CHUNKS,)),
-                dma((4, CHUNKS)),
+                dma((2 * CHUNKS,)), dma((4, CHUNKS)),
+                dma((3, 4)), dma((3, 4)),
+                dma, dma,
                 dma((3, 4)), dma((3, 4)),
                 dma, dma,
             ],

time: 174 us -> 138 us (0.79)
  the two profiles are of different devices: /device:TPU:61 before, /device:TPU:62 now
where the time goes in v2:
time: 138 us; the launch traced here: 135 us
  Pallas kernels  133 us (96%)
  local copies, waits for them, and re-layouts  1.45 us (1%)
    pallas_call x1, Pallas kernels, body(): pl.pallas_call(kernel, out_shape=(whole, plane, plane, plane, plane, jax....  119 us
    pallas_call x1, Pallas kernels, body(): pl.pallas_call(apply_kernel, out_shape=(whole, whole), in_specs=[anywhere...  14.2 us

profile of v2, /device:TPU:62, one launch (start us, length us, event | category | flops | bytes accessed | tf_op | source)
XLA Modules:
  0.0 135.3 jit_solution(982251798028589402)
XLA Ops:
  0.6 0.0 copy-start
  0.6 0.8 copy-done
  1.5 119.0 %exchange.1 = (f32[64,16384]{1,0:T(8,128)}, f32[64,8192]{1,0:T(8,128)S(1)}, f32[64,8192]{1,0:T(8,128)S(1)}, f32[64,8192]{1,0:T(8,128)}, f32[64,8192]{1,0:T(8,128...) custom-call(f32[64,16384]{1,0:T(8,128)} %bitcast.8, f32[1,16384]{1,0:T(1,128)S(1)} %bitcast.5), custom_call_target="tpu_custom_call" | custom-call | tf_op jit(solution)/shard_map/exchange/pallas_call | solution.py:547
  120.5 14.2 %apply.1 = (f32[64,16384]{1,0:T(8,128)}, f32[64,16384]{1,0:T(8,128)}) custom-call(f32[64,16384]{1,0:T(8,128)} %bitcast.9, f32[64,16384]{1,0:T(8,128)} %get-tuple-element.12.prev_h, f32[64,8192]{1,0:T(8,128)S(1)} %get-tuple-element.13.low_h, f32[64,8192]{1,0:T(8,128)S(1)} %get-tuple-element.14.high_h, f32[64,8192]{1,0:T(8,128)} %get-tuple-element.15.plow_h, ...), custom_call_target="tpu_custom_call" | custom-call | tf_op jit(solution)/shard_map/apply/pallas_call | solution.py:586
  134.7 0.6 copy.6
Async XLA Ops:
  0.6 0.8 copy-start

commit v3 on v2

--- a/solution.py
+++ b/solution.py
@@ -14,12 +14,12 @@
 LANES = 128
 LAYER = 16
 CHUNKS = 8
-RELAYS = {0: 3, 1: 7, 2: 10, 5: 9, 6: 13, 7: 8}
-OWN, STRAIGHT = 3, 4
-FIRST_CROSS, THEN_CROSS = (6,), (0, 2, 3, 1, 7, 4, 5)
+RELAYS = {0: 3, 1: 7, 2: 10, 5: 14, 6: 13, 7: 8}
+LANDING = 4
+FIRST_CROSS, THEN_CROSS = (6, 5), (4, 2, 0, 1, 3, 7)
 ACROSS, BESIDE = (2, 5, 7), (0, 1, 3, 4, 6)
 FIRST_ONWARD, NEXT_ONWARD = 2, 4
-INVERT_AT = 4
+INVERT_AT = 5
 
 
 def split(v):
@@ -211,18 +211,17 @@
     base = layer * LAYER
 
     def up_cross(c):
-        if c == STRAIGHT:
+        if c not in RELAYS and c != LANDING:
             return up_plain(c)
-        dst, recv, to = (up_b, 1, r + LAYER) if c == OWN else (up_a, 0, base + RELAYS[c])
-        return remote(x.at[:, at(CHUNKS + c)], dst, up_send.at[c], relay_recv.at[recv], i, to)
+        return remote(
+            x.at[:, at(CHUNKS + c)], up_a, up_send.at[c], relay_recv.at[0], i, base + RELAYS.get(c, 0))
 
     def down_cross(c):
-        if c == STRAIGHT:
+        if c not in RELAYS and c != LANDING:
             return down_plain(c)
-        dst, recv, to = (
-            (down_b, 3, r - LAYER) if c == OWN else (down_a, 2, base + LAYER - 1 - RELAYS[c])
-        )
-        return remote(x.at[:, at(c)], dst, down_send.at[c], relay_recv.at[recv], i, to)
+        return remote(
+            x.at[:, at(c)], down_a, down_send.at[c], relay_recv.at[2],
+            i, base + LAYER - 1 - RELAYS.get(c, 0))
 
     def onward(c):
         return remote(x.at[:, at(c)], prev.at[:, at(c)], x_send.at[c], x_recv.at[c], i + 1, r)
@@ -278,22 +277,25 @@
         for c, of in RELAYS.items():
             chunk = chunk + jnp.where(column == of, c, 0)
             first = jnp.logical_or(first, column == of)
-        own = column == LAYER - 1
-        return chunk + jnp.where(own, OWN, 0), first, jnp.logical_or(first, own)
-
-    up_chunk, up_first, up_second = role(q)
-    down_chunk, down_first, down_second = role(LAYER - 1 - q)
+        return chunk, first
+
+    up_chunk, up_relay = role(q)
+    down_chunk, down_relay = role(LAYER - 1 - q)
     above, below = layer < layers - 1, layer > 0
     first_hops = (
-        (jnp.logical_and(up_first, above), 0, up_a, remote(
+        (jnp.logical_and(up_relay, above), 0, up_a, remote(
             up_a, up_b, relay_send.at[0], relay_recv.at[1], i, r + LAYER)),
-        (jnp.logical_and(down_first, below), 2, down_a, remote(
+        (jnp.logical_and(down_relay, below), 2, down_a, remote(
             down_a, down_b, relay_send.at[2], relay_recv.at[3], i, r - LAYER)),
+        (jnp.logical_and(first_of_layer, above), 0, up_a, remote(
+            up_a, low.at[:, at(LANDING)], relay_send.at[0], low_recv.at[LANDING], i, r + LAYER)),
+        (jnp.logical_and(last_of_layer, below), 2, down_a, remote(
+            down_a, high.at[:, at(LANDING)], relay_send.at[2], high_recv.at[LANDING], i, r - LAYER)),
     )
     second_hops = (
-        (jnp.logical_and(up_second, below), 1, up_b, remote(
+        (jnp.logical_and(up_relay, below), 1, up_b, remote(
             up_b, low.at[:, at(up_chunk)], relay_send.at[1], low_recv.at[up_chunk], i, base)),
-        (jnp.logical_and(down_second, above), 3, down_b, remote(
+        (jnp.logical_and(down_relay, above), 3, down_b, remote(
             down_b, high.at[:, at(down_chunk)], relay_send.at[3], high_recv.at[down_chunk],
             i, base + LAYER - 1)),
     )
@@ -408,17 +410,36 @@
     start_chunks(jnp.logical_not(has_prev), (none_low, none_high), range(CHUNKS))
     start_chunks(all_of(lone, jnp.logical_not(has_low)), (own_low,), BESIDE)
     start_chunks(all_of(lone, jnp.logical_not(has_high)), (own_high,), BESIDE)
+    passes = (
+        (all_of(lone, qy < 3), pass_up, BESIDE),
+        (all_of(lone, q == LAYER - 2, above), pass_up, ACROSS),
+        (all_of(lone, qy > 0), pass_down, BESIDE),
+        (all_of(lone, q == 1, below), pass_down, ACROSS),
+        (all_of(lone, qy == 3, plain_up), pass_up, BESIDE),
+        (all_of(lone, qy == 0, plain_down), pass_down, BESIDE),
+    )
+    only_high, only_low = jnp.logical_and(across, cross_up), jnp.logical_and(across, cross_down)
+    not_up = jnp.logical_and(across, jnp.logical_not(cross_up))
+    not_down = jnp.logical_and(across, jnp.logical_not(cross_down))
+
     sum_start(*late, 0, partial)
+    for there, copy, chunks in passes[:4]:
+        start_chunks(there, (copy,), chunks)
     pl.when(lone)(invert)
     partial = sum_end(*late, 0)
     partial = summed(1, partial)
-    partial = summed(2, partial)
-    total[...] = partial
+    for there, copy, chunks in passes[4:]:
+        start_chunks(there, (copy,), chunks)
+    sum_start(*late, 2, partial)
+    start_chunks(not_up, (give_low,), ACROSS[:1])
+    start_chunks(not_down, (give_high,), ACROSS[:1])
+    total[...] = sum_end(*late, 2)
     hand = remote(total.at[pl.ds(0, n)], prior, prior_send, prior_recv, i + 1, r)
     pl.when(has_next)(lambda: hand.start())
-    start_chunks(all_of(lone, has_high), (pass_up,), BESIDE)
-    start_chunks(all_of(lone, has_low), (pass_down,), BESIDE)
-    start_chunks(across, (give_low, give_high), ACROSS)
+    start_chunks(not_up, (give_low,), ACROSS[1:])
+    start_chunks(not_down, (give_high,), ACROSS[1:])
+    start_chunks(only_low, (give_low,), BESIDE)
+    start_chunks(only_high, (give_high,), BESIDE)
     wait_prior = lambda: pl.when(has_prev)(lambda: hand.wait_recv())
     coefficients(total[...], inv_p[...], prior, wait_prior, w_o, r_o)
 
@@ -441,9 +462,12 @@
     pl.when(has_next)(lambda: early_hand.wait_send())
     end_chunks(has_next, (onward,), range(2 * CHUNKS))
     end_chunks(gives, (give_low, give_high), range(CHUNKS))
-    end_chunks(across, (give_low, give_high), ACROSS)
-    end_chunks(all_of(lone, has_high), (pass_up,), BESIDE)
-    end_chunks(all_of(lone, has_low), (pass_down,), BESIDE)
+    end_chunks(not_up, (give_low,), ACROSS)
+    end_chunks(not_down, (give_high,), ACROSS)
+    end_chunks(only_low, (give_low,), BESIDE)
+    end_chunks(only_high, (give_high,), BESIDE)
+    for there, copy, chunks in passes:
+        end_chunks(there, (copy,), chunks)
     for there, _, _, copy in first_hops + second_hops:
         pl.when(there)(lambda copy=copy: copy.wait_send())
 

time: 138 us -> 127 us (0.920); the launches traced: 135 us -> 127 us
  Pallas kernels: 133 us -> 125 us
    pallas_call x1, Pallas kernels: 119 us -> 110 us  [body(): pl.pallas_call(kernel, out_shape=(whole, plane, plane, plane, plane, jax....]
where the time goes in v3:
time: 127 us
  Pallas kernels  125 us (98%)
  local copies, waits for them, and re-layouts  1.45 us (1%)
    pallas_call x1, Pallas kernels, body(): pl.pallas_call(kernel, out_shape=(whole, plane, plane, plane, plane, jax....  110 us
    pallas_call x1, Pallas kernels, body(): pl.pallas_call(apply_kernel, out_shape=(whole, whole), in_specs=[anywhere...  14.2 us

profile of v3, /device:TPU:62, one launch (start us, length us, event | category | flops | bytes accessed | tf_op | source)
XLA Modules:
  0.0 126.7 jit_solution(5308887120197942343)
XLA Ops:
  0.6 0.0 copy-start
  0.6 0.8 copy-done
  1.5 110.4 %exchange.1 = (f32[64,16384]{1,0:T(8,128)}, f32[64,8192]{1,0:T(8,128)S(1)}, f32[64,8192]{1,0:T(8,128)S(1)}, f32[64,8192]{1,0:T(8,128)}, f32[64,8192]{1,0:T(8,128...) custom-call(f32[64,16384]{1,0:T(8,128)} %bitcast.8, f32[1,16384]{1,0:T(1,128)S(1)} %bitcast.5), custom_call_target="tpu_custom_call" | custom-call | tf_op jit(solution)/shard_map/exchange/pallas_call | solution.py:571
  111.9 14.2 %apply.1 = (f32[64,16384]{1,0:T(8,128)}, f32[64,16384]{1,0:T(8,128)}) custom-call(f32[64,16384]{1,0:T(8,128)} %bitcast.9, f32[64,16384]{1,0:T(8,128)} %get-tuple-element.12.prev_h, f32[64,8192]{1,0:T(8,128)S(1)} %get-tuple-element.13.low_h, f32[64,8192]{1,0:T(8,128)S(1)} %get-tuple-element.14.high_h, f32[64,8192]{1,0:T(8,128)} %get-tuple-element.15.plow_h, ...), custom_call_target="tpu_custom_call" | custom-call | tf_op jit(solution)/shard_map/apply/pallas_call | solution.py:610
  126.1 0.6 copy.6
Async XLA Ops:
  0.6 0.8 copy-start

commit v4 on v3

--- a/solution.py
+++ b/solution.py
@@ -12,9 +12,11 @@
 BF16 = jnp.bfloat16
 
 LANES = 128
+VMEM_EXCHANGE, VMEM_APPLY = 16 * 2**20, 8 * 2**20
 LAYER = 16
 CHUNKS = 8
-RELAYS = {0: 3, 1: 7, 2: 10, 5: 14, 6: 13, 7: 8}
+RELAYS_UP = {0: 3, 1: 7, 2: 10, 5: 14, 6: 13, 7: 11}
+RELAYS_DOWN = {0: 12, 1: 8, 2: 5, 5: 1, 6: 2, 7: 10}
 LANDING = 4
 FIRST_CROSS, THEN_CROSS = (6, 5), (4, 2, 0, 1, 3, 7)
 ACROSS, BESIDE = (2, 5, 7), (0, 1, 3, 4, 6)
@@ -63,11 +65,16 @@
     row = lax.broadcasted_iota(jnp.int32, (n, LANES), 0)
     lane = lax.broadcasted_iota(jnp.int32, (n, LANES), 1)
     t = jnp.where(lane < n, square, jnp.where(lane == row + n, 1.0, 0.0))
-    for k in range(n):
-        pivot = t[k : k + 1, :]
-        scaled = pivot * (1.0 / t[k : k + 1, k : k + 1])
-        column = jnp.where(row > k, jnp.broadcast_to(t[:, k : k + 1], (n, LANES)), 0.0)
-        t = t - column * scaled
+    for k in range(0, n, 2):
+        top, under = t[k : k + 1, :], t[k + 1 : k + 2, :]
+        one = 1.0 / t[k : k + 1, k : k + 1]
+        ratio = t[k + 1 : k + 2, k : k + 1] * one
+        first = jnp.broadcast_to(t[:, k : k + 1], (n, LANES))
+        second = jnp.broadcast_to(t[:, k + 1 : k + 2], (n, LANES)) - first * ratio
+        under = under - top * ratio
+        two = 1.0 / (t[k + 1 : k + 2, k + 1 : k + 2] - t[k : k + 1, k + 1 : k + 2] * ratio)
+        t = t - jnp.where(row > k, first, 0.0) * (top * one)
+        t = t - jnp.where(row > k + 1, second, 0.0) * (under * two)
     diagonal = jnp.sum(jnp.where(lane == row, t, 0.0), axis=1, keepdims=True)
     t = t * (1.0 / jnp.sqrt(diagonal))
     return pltpu.roll(t, LANES - n, 1)[:, :n]
@@ -100,12 +107,12 @@
 
 def exchange_kernel(
     intervals, rows,
-    x_h, pot,
-    prev_o, low_o, high_o, plow_o, phigh_o, w_o, r_o,
-    x, prev, low, high, up_a, up_b, down_a, down_b, acc, sums, total, prior, early_sums, early_total, early_prior, inv_p,
+    x, pot,
+    prev, z_hi, z_lo, plow_o, phigh_o, w_o, r_o,
+    low, high, up_a, up_b, down_a, down_b, acc, sums, total, prior, early_sums, early_total, early_prior, inv_p,
     x_send, x_recv, up_send, down_send, low_recv, high_recv,
     relay_send, relay_recv, pass_up_send, pass_down_send, plow_send, phigh_send, plow_recv, phigh_recv,
-    in_sem, out_sem, sum_send, sum_recv, prior_send, prior_recv,
+    sum_send, sum_recv, prior_send, prior_recv,
     early_send, early_recv, early_prior_send, early_prior_recv,
 ):
     i, r = lax.axis_index("interval"), lax.axis_index("rows")
@@ -123,12 +130,6 @@
             src_ref=src, dst_ref=dst, send_sem=send, recv_sem=recv,
             device_id=(to_i, to_r), device_id_type=MESH,
         )
-
-    loads = [
-        pltpu.make_async_copy(x_h.at[:, at(c)], x.at[:, at(c)], in_sem.at[c]) for c in range(2 * CHUNKS)
-    ]
-    for copy in loads:
-        copy.start()
 
     barrier = pltpu.get_barrier_semaphore()
 
@@ -149,8 +150,6 @@
         has_prev.astype(jnp.int32) + has_next.astype(jnp.int32)
         + has_low.astype(jnp.int32) + has_high.astype(jnp.int32)
     )
-    for copy in loads:
-        copy.wait()
     n = prior.shape[0]
     early_acc = acc.at[pl.ds(0, 2 * n), pl.ds(0, 2 * n)]
     early_acc[...] = jnp.zeros((2 * n, 2 * n), F32)
@@ -211,17 +210,17 @@
     base = layer * LAYER
 
     def up_cross(c):
-        if c not in RELAYS and c != LANDING:
+        if c not in RELAYS_UP and c != LANDING:
             return up_plain(c)
         return remote(
-            x.at[:, at(CHUNKS + c)], up_a, up_send.at[c], relay_recv.at[0], i, base + RELAYS.get(c, 0))
+            x.at[:, at(CHUNKS + c)], up_a, up_send.at[c], relay_recv.at[0], i, base + RELAYS_UP.get(c, 0))
 
     def down_cross(c):
-        if c not in RELAYS and c != LANDING:
+        if c not in RELAYS_DOWN and c != LANDING:
             return down_plain(c)
         return remote(
             x.at[:, at(c)], down_a, down_send.at[c], relay_recv.at[2],
-            i, base + LAYER - 1 - RELAYS.get(c, 0))
+            i, base + RELAYS_DOWN.get(c, LAYER - 1))
 
     def onward(c):
         return remote(x.at[:, at(c)], prev.at[:, at(c)], x_send.at[c], x_recv.at[c], i + 1, r)
@@ -272,15 +271,15 @@
     def _():
         high[...] = jnp.zeros_like(high)
 
-    def role(column):
+    def role(table):
         chunk, first = jnp.int32(0), jnp.bool_(False)
-        for c, of in RELAYS.items():
-            chunk = chunk + jnp.where(column == of, c, 0)
-            first = jnp.logical_or(first, column == of)
+        for c, of in table.items():
+            chunk = chunk + jnp.where(q == of, c, 0)
+            first = jnp.logical_or(first, q == of)
         return chunk, first
 
-    up_chunk, up_relay = role(q)
-    down_chunk, down_relay = role(LAYER - 1 - q)
+    up_chunk, up_relay = role(RELAYS_UP)
+    down_chunk, down_relay = role(RELAYS_DOWN)
     above, below = layer < layers - 1, layer > 0
     first_hops = (
         (jnp.logical_and(up_relay, above), 0, up_a, remote(
@@ -331,24 +330,18 @@
     def give_high(c):
         return remote(high.at[:, at(c)], phigh_o.at[:, at(c)], phigh_send.at[c], phigh_recv.at[c], i + 1, r)
 
-    def writes(c):
-        return (
-            pltpu.make_async_copy(prev.at[:, at(c)], prev_o.at[:, at(c)], out_sem.at[0, c]),
-            pltpu.make_async_copy(
-                prev.at[:, at(CHUNKS + c)], prev_o.at[:, at(CHUNKS + c)], out_sem.at[1, c]),
-            pltpu.make_async_copy(low.at[:, at(c)], low_o.at[:, at(c)], out_sem.at[2, c]),
-            pltpu.make_async_copy(high.at[:, at(c)], high_o.at[:, at(c)], out_sem.at[3, c]),
-        )
-
     lone = jnp.logical_and(has_prev, gives)
 
     def invert():
         pl.when(has_prev)(lambda: early_hand.wait_recv())
         inv_p[...] = inverse_factor(early_prior[...])
 
+    crossed = jnp.logical_or(cross_up, cross_down).astype(jnp.int32)
+
     @pl.loop(0, CHUNKS)
-    def _(c):
-        pl.when(jnp.logical_and(c == INVERT_AT, jnp.logical_not(lone)))(invert)
+    def _(step):
+        c = lax.rem(step + crossed, CHUNKS)
+        pl.when(jnp.logical_and(step == INVERT_AT, jnp.logical_not(lone)))(invert)
 
         @pl.when(has_prev)
         def _():
@@ -362,9 +355,6 @@
         @pl.when(has_high)
         def _():
             down_plain(c).wait_recv()
-
-        for copy in writes(c):
-            copy.start()
 
         @pl.when(gives)
         def _():
@@ -378,6 +368,9 @@
             mine_hi, mine_lo = split(mine)
             image_hi, image_lo = split(image)
             theirs_hi, theirs_lo = split(theirs)
+            where = at(plane * CHUNKS + c)
+            z_hi[:, where] = jnp.concatenate([mine_hi, theirs_hi, image_hi], axis=0)
+            z_lo[:, where] = jnp.concatenate([mine_lo, theirs_lo, image_lo], axis=0)
             left = jnp.concatenate([mine_hi, theirs_hi, mine_lo, theirs_lo], axis=0)
             right = jnp.concatenate([mine_hi, image_hi, mine_lo, image_lo], axis=0)
             acc[...] += lax.dot_general(
@@ -425,6 +418,8 @@
     sum_start(*late, 0, partial)
     for there, copy, chunks in passes[:4]:
         start_chunks(there, (copy,), chunks)
+    start_chunks(only_low, (give_low,), BESIDE[:2])
+    start_chunks(only_high, (give_high,), BESIDE[:2])
     pl.when(lone)(invert)
     partial = sum_end(*late, 0)
     partial = summed(1, partial)
@@ -438,14 +433,12 @@
     pl.when(has_next)(lambda: hand.start())
     start_chunks(not_up, (give_low,), ACROSS[1:])
     start_chunks(not_down, (give_high,), ACROSS[1:])
-    start_chunks(only_low, (give_low,), BESIDE)
-    start_chunks(only_high, (give_high,), BESIDE)
+    start_chunks(only_low, (give_low,), BESIDE[2:])
+    start_chunks(only_high, (give_high,), BESIDE[2:])
     wait_prior = lambda: pl.when(has_prev)(lambda: hand.wait_recv())
     coefficients(total[...], inv_p[...], prior, wait_prior, w_o, r_o)
 
     for c in range(CHUNKS):
-        for copy in writes(c):
-            copy.wait()
         give_low(c).wait_recv()
         give_high(c).wait_recv()
 
@@ -478,29 +471,16 @@
 
 
 def apply_kernel(
-    x_h, prev_h, low_h, high_h, plow_h, phigh_h, pot, w, basis_o, residual_o,
-    x, prev, low, high, plow, phigh, out, in_sem, out_sem,
+    prev, z_hi, z_lo, plow, phigh, pot, w, r, basis_o, ritz_o, residual_o, out, out_sem, ritz_sem
 ):
-    size = low.shape[1]
+    size = plow.shape[1]
     width = size // CHUNKS
-    n = x.shape[0]
+    n = prev.shape[0]
+    ritz = pltpu.make_async_copy(r, ritz_o, ritz_sem)
+    ritz.start()
 
     def at(c):
         return pl.ds(pl.multiple_of(c * width, LANES), width)
-
-    def reads(c):
-        pairs = (
-            (x_h, x, c), (x_h, x, CHUNKS + c), (prev_h, prev, c), (prev_h, prev, CHUNKS + c),
-            (low_h, low, c), (high_h, high, c), (plow_h, plow, c), (phigh_h, phigh, c),
-        )
-        return [
-            pltpu.make_async_copy(src.at[:, at(k)], dst.at[:, at(k)], in_sem.at[e, c])
-            for e, (src, dst, k) in enumerate(pairs)
-        ]
-
-    for c in range(CHUNKS):
-        for copy in reads(c):
-            copy.start()
 
     def writes(plane, c):
         where = at(plane * CHUNKS + c)
@@ -511,30 +491,19 @@
 
     w_hi, w_lo = split(w[...])
     both = jnp.concatenate([w_hi, w_lo], axis=0)
-    for copy in reads(0):
-        copy.wait()
 
     @pl.loop(0, CHUNKS)
     def _(c):
-        @pl.when(c < CHUNKS - 1)
-        def _():
-            for copy in reads(c + 1):
-                copy.wait()
-
         for plane in range(2):
-            k = plane * CHUNKS + c
-            z = jnp.concatenate(
-                [
-                    x[:, at(k)],
-                    prev[:, at(k)],
-                    stencil(x, low, high, pot, plane, c, size, width),
-                    stencil(prev, plow, phigh, pot, plane, c, size, width),
-                ],
-                axis=0,
+            where = at(plane * CHUNKS + c)
+            image_hi, image_lo = split(stencil(prev, plow, phigh, pot, plane, c, size, width))
+            wide = jnp.dot(
+                both, jnp.concatenate([z_hi[:, where], image_hi], axis=0), preferred_element_type=F32
             )
-            z_hi, z_lo = split(z)
-            wide = jnp.dot(both, z_hi, preferred_element_type=F32)
-            value = (wide[: 2 * n] + wide[2 * n :]) + jnp.dot(w_hi, z_lo, preferred_element_type=F32)
+            narrow = jnp.dot(
+                w_hi, jnp.concatenate([z_lo[:, where], image_lo], axis=0), preferred_element_type=F32
+            )
+            value = (wide[: 2 * n] + wide[2 * n :]) + narrow
 
             @pl.when(c > 0)
             def _():
@@ -548,6 +517,7 @@
     for plane in range(2):
         for copy in writes(plane, CHUNKS - 1):
             copy.wait()
+    ritz.wait()
 
 
 def solution(mesh):
@@ -559,7 +529,7 @@
         size = cells // 2
         width = size // CHUNKS
         pot = potential.reshape(1, cells)
-        anywhere = pl.BlockSpec(memory_space=pl.ANY)
+        hbm = pl.BlockSpec(memory_space=pltpu.HBM)
         vmem = pl.BlockSpec(memory_space=pltpu.VMEM)
         whole = jax.ShapeDtypeStruct((n, cells), F32)
         plane = jax.ShapeDtypeStruct((n, size), F32)
@@ -568,18 +538,17 @@
         def kernel(*refs):
             exchange_kernel(intervals, rows, *refs)
 
-        prev, low, high, plow, phigh, w, ritz = pl.pallas_call(
+        stack = jax.ShapeDtypeStruct((3 * n, cells), BF16)
+        prev, z_hi, z_lo, plow, phigh, w, r = pl.pallas_call(
             kernel,
             out_shape=(
-                whole, plane, plane, plane, plane,
+                whole, stack, stack, plane, plane,
                 jax.ShapeDtypeStruct((2 * n, 4 * n), F32),
                 jax.ShapeDtypeStruct((n, n), F32),
             ),
-            in_specs=[anywhere, vmem],
-            out_specs=(anywhere,) * 5 + (vmem, vmem),
+            in_specs=[vmem, vmem],
+            out_specs=(vmem,) * 7,
             scratch_shapes=[
-                pltpu.VMEM((n, cells), F32),
-                pltpu.VMEM((n, cells), F32),
                 pltpu.VMEM((n, size), F32),
                 pltpu.VMEM((n, size), F32),
                 *[pltpu.VMEM((n, width), F32) for _ in range(4)],
@@ -596,32 +565,25 @@
                 dma((4,)), dma((4,)),
                 dma((CHUNKS,)), dma((CHUNKS,)),
                 dma((CHUNKS,)), dma((CHUNKS,)), dma((CHUNKS,)), dma((CHUNKS,)),
-                dma((2 * CHUNKS,)), dma((4, CHUNKS)),
                 dma((3, 4)), dma((3, 4)),
                 dma, dma,
                 dma((3, 4)), dma((3, 4)),
                 dma, dma,
             ],
             compiler_params=pltpu.CompilerParams(
-                collective_id=0, has_side_effects=True, vmem_limit_bytes=48 * 2**20
+                collective_id=0, has_side_effects=True, vmem_limit_bytes=VMEM_EXCHANGE
             ),
             name="exchange",
         )(x, pot)
-        basis, residual = pl.pallas_call(
+        basis, ritz, residual = pl.pallas_call(
             apply_kernel,
-            out_shape=(whole, whole),
-            in_specs=[anywhere] * 6 + [vmem, vmem],
-            out_specs=(anywhere, anywhere),
-            scratch_shapes=[
-                pltpu.VMEM((n, cells), F32),
-                pltpu.VMEM((n, cells), F32),
-                *[pltpu.VMEM((n, size), F32) for _ in range(4)],
-                pltpu.VMEM((2, 2 * n, width), F32),
-                dma((8, CHUNKS)), dma((2, 2)),
-            ],
-            compiler_params=pltpu.CompilerParams(vmem_limit_bytes=48 * 2**20),
+            out_shape=(whole, jax.ShapeDtypeStruct((n, n), F32), whole),
+            in_specs=[vmem] * 8,
+            out_specs=(hbm,) * 3,
+            scratch_shapes=[pltpu.VMEM((2, 2 * n, width), F32), dma((2, 2)), dma],
+            compiler_params=pltpu.CompilerParams(vmem_limit_bytes=VMEM_APPLY),
             name="apply",
-        )(x, prev, low, high, plow, phigh, pot, w)
+        )(prev, z_hi, z_lo, plow, phigh, pot, w, r)
         return basis[None], ritz[None], residual[None]
 
     return jax.shard_map(

time: 127 us -> 114 us (0.90)
  the two profiles are of different devices: /device:TPU:62 before, /device:TPU:1 now
where the time goes in v4:
time: 114 us
  Pallas kernels  110 us (96%)
  local copies, waits for them, and re-layouts  3.02 us (3%)
    pallas_call x1, Pallas kernels, body(): pl.pallas_call(kernel, out_shape=(whole, stack, stack, plane, plane, jax....  101 us
    pallas_call x1, Pallas kernels, body(): pl.pallas_call(apply_kernel, out_shape=(whole, jax.ShapeDtypeStruct((n, n...  9.2 us
    unnamed x4, local copies, waits for them, and re-layouts  3.02 us

profile of v4, /device:TPU:1, one launch (start us, length us, event | category | flops | bytes accessed | tf_op | source)
XLA Modules:
  0.0 113.9 jit_solution(11045060420719266625)
XLA Ops:
  0.6 0.0 copy-start
  0.6 2.2 %copy-done = f32[1,64,16384]{2,1,0:T(8,128)S(1)} copy-done((f32[1,64,16384]{2,1,0:T(8,128)S(1)}, f32[1,64,16384]{2,1,0:T(8,128)}, u32[]{:S(2)}) %copy-start) | copy-done | bytes 4194328
  2.8 0.0 copy-start.1
  2.8 0.8 copy-done.1
  3.7 101.0 %exchange.1 = (f32[64,16384]{1,0:T(8,128)S(1)}, bf16[192,16384]{1,0:T(8,128)(2,1)S(1)}, bf16[192,16384]{1,0:T(8,128)(2,1)S(1)}, f32[64,8192]{1,0:T(8,128)S(1)}, ...) custom-call(f32[64,16384]{1,0:T(8,128)S(1)} %bitcast.5, f32[1,16384]{1,0:T(1,128)S(1)} %bitcast.6), custom_call_target="tpu_custom_call" | custom-call | tf_op jit(solution)/shard_map/exchange/pallas_call | solution.py:542
  104.7 9.2 %apply.1 = (f32[64,16384]{1,0:T(8,128)}, f32[64,64]{1,0:T(8,128)}, f32[64,16384]{1,0:T(8,128)}) custom-call(f32[64,16384]{1,0:T(8,128)S(1)} %get-tuple-element.13.prev, bf16[192,16384]{1,0:T(8,128)(2,1)S(1)} %get-tuple-element.14.z_hi, bf16[192,16384]{1,0:T(8,128)(2,1)S(1)} %get-tuple-element.15.z_lo, f32[64,8192]{1,0:T(8,128)S(1)} %get-tuple-element.16.plow, ...), custom_call_target="tpu_custom_call" | custom-call | tf_op jit(solution)/shard_map/apply/pallas_call | solution.py:578
Async XLA Ops:
  0.6 2.2 %copy-start = (f32[1,64,16384]{2,1,0:T(8,128)S(1)}, f32[1,64,16384]{2,1,0:T(8,128)}, u32[]{:S(2)}) copy-start(f32[1,64,16384]{2,1,0:T(8,128)} %param.2) | copy-start | bytes 12582916
  2.8 0.8 copy-start.1

commit v5 on v4

--- a/solution.py
+++ b/solution.py
@@ -65,26 +65,44 @@
     row = lax.broadcasted_iota(jnp.int32, (n, LANES), 0)
     lane = lax.broadcasted_iota(jnp.int32, (n, LANES), 1)
     t = jnp.where(lane < n, square, jnp.where(lane == row + n, 1.0, 0.0))
+    rows = [t[b : b + 8] for b in range(0, n, 8)]
+    shape = (8, LANES)
+    place = lax.broadcasted_iota(jnp.int32, shape, 0)
     for k in range(0, n, 2):
-        top, under = t[k : k + 1, :], t[k + 1 : k + 2, :]
-        one = 1.0 / t[k : k + 1, k : k + 1]
-        ratio = t[k + 1 : k + 2, k : k + 1] * one
-        first = jnp.broadcast_to(t[:, k : k + 1], (n, LANES))
-        second = jnp.broadcast_to(t[:, k + 1 : k + 2], (n, LANES)) - first * ratio
+        at, own = k % 8, rows[k // 8]
+        top, under = own[at : at + 1, :], own[at + 1 : at + 2, :]
+        one = 1.0 / own[at : at + 1, k : k + 1]
+        ratio = own[at + 1 : at + 2, k : k + 1] * one
         under = under - top * ratio
-        two = 1.0 / (t[k + 1 : k + 2, k + 1 : k + 2] - t[k : k + 1, k + 1 : k + 2] * ratio)
-        t = t - jnp.where(row > k, first, 0.0) * (top * one)
-        t = t - jnp.where(row > k + 1, second, 0.0) * (under * two)
+        two = 1.0 / (own[at + 1 : at + 2, k + 1 : k + 2] - own[at : at + 1, k + 1 : k + 2] * ratio)
+        scaled, scaled_under = top * one, under * two
+        for b in range(k // 8, n // 8):
+            first = jnp.broadcast_to(rows[b][:, k : k + 1], shape)
+            second = jnp.broadcast_to(rows[b][:, k + 1 : k + 2], shape) - first * ratio
+            if b == k // 8:
+                first = jnp.where(place > at, first, 0.0)
+                second = jnp.where(place > at + 1, second, 0.0)
+            rows[b] = rows[b] - first * scaled - second * scaled_under
+    t = jnp.concatenate(rows, axis=0)
     diagonal = jnp.sum(jnp.where(lane == row, t, 0.0), axis=1, keepdims=True)
     t = t * (1.0 / jnp.sqrt(diagonal))
     return pltpu.roll(t, LANES - n, 1)[:, :n]
 
 
-def coefficients(total, inv_p, prior, wait_prior, w_out, r_out):
-    n = total.shape[0] // 2
-    swapped = pltpu.roll(total, n, 1)
-    gram, k_own = total[:n, :n], swapped[:n, :n]
-    g_pi, k_pi = total[n:, :n], swapped[n:, :n]
+def pack(upper, lower):
+    lane = lax.broadcasted_iota(jnp.int32, upper.shape, 1)
+    return jnp.where(lane < LANES // 2, upper, lower)
+
+
+def unpack(packed):
+    return jnp.concatenate([packed, pltpu.roll(packed, LANES // 2, 1)], axis=0)
+
+
+def coefficients(own, total, inv_p, prior, wait_prior, w_out, r_out):
+    n = total.shape[0] - own.shape[0]
+    gram = unpack(own)[:, :n]
+    g_pi, k_pi = total[:n, :n], pltpu.roll(total[:n], n, 1)[:, :n]
+    k_own = unpack(total[n:])[:, :n]
     et = exact_dot(inv_p, g_pi, ((1,), (0,)))
     schur = gram - exact_dot(et, et, ((0,), (0,)))
     toward = exact_dot(et, inv_p, ((0,), (0,)))
@@ -95,7 +113,7 @@
     ritz = exact_dot(exact_dot(a, k_own, ((1,), (0,))), a, ((1,), (1,)))
     ritz = ritz + exact_dot(mixed, a, ((1,), (1,))) + exact_dot(a, mixed, ((1,), (1,)))
     wait_prior()
-    k_prior = pltpu.roll(prior[...], n, 1)[:, :n]
+    k_prior = unpack(prior[...])[:, :n]
     ritz = ritz + exact_dot(exact_dot(b, k_prior, ((1,), (0,))), b, ((1,), (1,)))
     r_out[...] = ritz
     ra = exact_dot(ritz, a, ((0,), (0,)))
@@ -150,7 +168,7 @@
         has_prev.astype(jnp.int32) + has_next.astype(jnp.int32)
         + has_low.astype(jnp.int32) + has_high.astype(jnp.int32)
     )
-    n = prior.shape[0]
+    n = acc.shape[0] // 4
     early_acc = acc.at[pl.ds(0, 2 * n), pl.ds(0, 2 * n)]
     early_acc[...] = jnp.zeros((2 * n, 2 * n), F32)
 
@@ -163,6 +181,7 @@
 
     halves = early_acc[pl.ds(0, n), :] + pltpu.roll(early_acc[pl.ds(n, n), :], n, 1)
     own_gram = halves + pltpu.roll(halves, n, 1)
+    own_gram = pack(own_gram[: n // 2], own_gram[n // 2 :])
     pl.semaphore_wait(barrier, layers - 1 + LAYER - 1 + neighbours)
 
     places = (
@@ -317,7 +336,7 @@
     def _():
         row = lax.broadcasted_iota(jnp.int32, early_prior.shape, 0)
         lane = lax.broadcasted_iota(jnp.int32, early_prior.shape, 1)
-        early_prior[...] = jnp.where(row == lane, 1.0, 0.0)
+        early_prior[...] = jnp.where(lax.rem(lane, n) == row + n // 2 * (lane // n), 1.0, 0.0)
         prior[...] = jnp.zeros_like(prior)
 
 
@@ -334,7 +353,7 @@
 
     def invert():
         pl.when(has_prev)(lambda: early_hand.wait_recv())
-        inv_p[...] = inverse_factor(early_prior[...])
+        inv_p[...] = inverse_factor(unpack(early_prior[...]))
 
     crossed = jnp.logical_or(cross_up, cross_down).astype(jnp.int32)
 
@@ -379,6 +398,8 @@
 
     half = acc.shape[0] // 2
     partial = acc[:half, :half] + acc[half:, half:] + (acc[:half, half:] + acc[half:, :half])
+    square = pltpu.roll(partial[: n // 2], n, 1)
+    partial = jnp.concatenate([partial[n:], pack(square, partial[n // 2 : n])], axis=0)
 
     def pass_up(c):
         return remote(
@@ -429,14 +450,14 @@
     start_chunks(not_up, (give_low,), ACROSS[:1])
     start_chunks(not_down, (give_high,), ACROSS[:1])
     total[...] = sum_end(*late, 2)
-    hand = remote(total.at[pl.ds(0, n)], prior, prior_send, prior_recv, i + 1, r)
+    hand = remote(total.at[pl.ds(n, n // 2)], prior, prior_send, prior_recv, i + 1, r)
     pl.when(has_next)(lambda: hand.start())
     start_chunks(not_up, (give_low,), ACROSS[1:])
     start_chunks(not_down, (give_high,), ACROSS[1:])
     start_chunks(only_low, (give_low,), BESIDE[2:])
     start_chunks(only_high, (give_high,), BESIDE[2:])
     wait_prior = lambda: pl.when(has_prev)(lambda: hand.wait_recv())
-    coefficients(total[...], inv_p[...], prior, wait_prior, w_o, r_o)
+    coefficients(early_total[...], total[...], inv_p[...], prior, wait_prior, w_o, r_o)
 
     for c in range(CHUNKS):
         give_low(c).wait_recv()
@@ -553,12 +574,12 @@
                 pltpu.VMEM((n, size), F32),
                 *[pltpu.VMEM((n, width), F32) for _ in range(4)],
                 pltpu.VMEM((4 * n, 4 * n), F32),
-                pltpu.VMEM((3, 4, 2 * n, 2 * n), F32),
-                pltpu.VMEM((2 * n, 2 * n), F32),
-                pltpu.VMEM((n, 2 * n), F32),
-                pltpu.VMEM((3, 4, n, 2 * n), F32),
-                pltpu.VMEM((n, 2 * n), F32),
-                pltpu.VMEM((n, 2 * n), F32),
+                pltpu.VMEM((3, 4, n + n // 2, 2 * n), F32),
+                pltpu.VMEM((n + n // 2, 2 * n), F32),
+                pltpu.VMEM((n // 2, 2 * n), F32),
+                pltpu.VMEM((3, 4, n // 2, 2 * n), F32),
+                pltpu.VMEM((n // 2, 2 * n), F32),
+                pltpu.VMEM((n // 2, 2 * n), F32),
                 pltpu.VMEM((n, n), F32),
                 dma((2 * CHUNKS,)), dma((2 * CHUNKS,)),
                 dma((CHUNKS,)), dma((CHUNKS,)), dma((CHUNKS,)), dma((CHUNKS,)),

time: 114 us -> 111 us (0.974)
  the two profiles are of different devices: /device:TPU:1 before, /device:TPU:62 now
where the time goes in v5:
time: 111 us; the launch traced here: 109 us
  Pallas kernels  106 us (95%)
  local copies, waits for them, and re-layouts  3.02 us (3%)
    pallas_call x1, Pallas kernels, body(): pl.pallas_call(kernel, out_shape=(whole, stack, stack, plane, plane, jax....  96.3 us
    pallas_call x1, Pallas kernels, body(): pl.pallas_call(apply_kernel, out_shape=(whole, jax.ShapeDtypeStruct((n, n...  9.2 us
    unnamed x4, local copies, waits for them, and re-layouts  3.02 us

profile of v5, /device:TPU:62, one launch (start us, length us, event | category | flops | bytes accessed | tf_op | source)
XLA Modules:
  0.0 109.2 jit_solution(6855463634960787815)
XLA Ops:
  0.6 0.0 copy-start
  0.6 2.2 %copy-done = f32[1,64,16384]{2,1,0:T(8,128)S(1)} copy-done((f32[1,64,16384]{2,1,0:T(8,128)S(1)}, f32[1,64,16384]{2,1,0:T(8,128)}, u32[]{:S(2)}) %copy-start) | copy-done | bytes 4194328
  2.8 0.0 copy-start.1
  2.8 0.8 copy-done.1
  3.7 96.3 %exchange.1 = (f32[64,16384]{1,0:T(8,128)S(1)}, bf16[192,16384]{1,0:T(8,128)(2,1)S(1)}, bf16[192,16384]{1,0:T(8,128)(2,1)S(1)}, f32[64,8192]{1,0:T(8,128)S(1)}, ...) custom-call(f32[64,16384]{1,0:T(8,128)S(1)} %bitcast.5, f32[1,16384]{1,0:T(1,128)S(1)} %bitcast.6), custom_call_target="tpu_custom_call" | custom-call | tf_op jit(solution)/shard_map/exchange/pallas_call | solution.py:563
  100.0 9.2 %apply.1 = (f32[64,16384]{1,0:T(8,128)}, f32[64,64]{1,0:T(8,128)}, f32[64,16384]{1,0:T(8,128)}) custom-call(f32[64,16384]{1,0:T(8,128)S(1)} %get-tuple-element.13.prev, bf16[192,16384]{1,0:T(8,128)(2,1)S(1)} %get-tuple-element.14.z_hi, bf16[192,16384]{1,0:T(8,128)(2,1)S(1)} %get-tuple-element.15.z_lo, f32[64,8192]{1,0:T(8,128)S(1)} %get-tuple-element.16.plow, ...), custom_call_target="tpu_custom_call" | custom-call | tf_op jit(solution)/shard_map/apply/pallas_call | solution.py:599
Async XLA Ops:
  0.6 2.2 %copy-start = (f32[1,64,16384]{2,1,0:T(8,128)S(1)}, f32[1,64,16384]{2,1,0:T(8,128)}, u32[]{:S(2)}) copy-start(f32[1,64,16384]{2,1,0:T(8,128)} %param.2) | copy-start | bytes 12582916
  2.8 0.8 copy-start.1

commit v6 on v5

--- a/solution.py
+++ b/solution.py
@@ -20,6 +20,7 @@
 LANDING = 4
 FIRST_CROSS, THEN_CROSS = (6, 5), (4, 2, 0, 1, 3, 7)
 ACROSS, BESIDE = (2, 5, 7), (0, 1, 3, 4, 6)
+NEAR, LAST = (0, 1, 2, 3, 4, 5, 6), (7,)
 FIRST_ONWARD, NEXT_ONWARD = 2, 4
 INVERT_AT = 5
 
@@ -425,37 +426,53 @@
     start_chunks(all_of(lone, jnp.logical_not(has_low)), (own_low,), BESIDE)
     start_chunks(all_of(lone, jnp.logical_not(has_high)), (own_high,), BESIDE)
     passes = (
-        (all_of(lone, qy < 3), pass_up, BESIDE),
-        (all_of(lone, q == LAYER - 2, above), pass_up, ACROSS),
-        (all_of(lone, qy > 0), pass_down, BESIDE),
-        (all_of(lone, q == 1, below), pass_down, ACROSS),
+        (all_of(lone, qy < 3), pass_up, NEAR),
+        (all_of(lone, q == LAYER - 2, above), pass_up, LAST),
+        (all_of(lone, qy > 0), pass_down, NEAR),
+        (all_of(lone, q == 1, below), pass_down, LAST),
         (all_of(lone, qy == 3, plain_up), pass_up, BESIDE),
         (all_of(lone, qy == 0, plain_down), pass_down, BESIDE),
     )
     only_high, only_low = jnp.logical_and(across, cross_up), jnp.logical_and(across, cross_down)
     not_up = jnp.logical_and(across, jnp.logical_not(cross_up))
     not_down = jnp.logical_and(across, jnp.logical_not(cross_down))
+    gifts = (
+        ((only_low, give_low, NEAR[:4]), (only_high, give_high, NEAR[:4])),
+        (
+            (only_low, give_low, NEAR[4:5]),
+            (only_high, give_high, NEAR[4:5]),
+            (all_of(not_up, not_down, qy == 0), give_low, ACROSS[:1]),
+            (all_of(not_up, not_down, qy == 3), give_high, ACROSS[:1]),
+            (all_of(not_up, qy > 0), give_low, LAST),
+            (all_of(not_down, qy < 3), give_high, LAST),
+        ),
+        (
+            (only_low, give_low, NEAR[5:] + LAST),
+            (only_high, give_high, NEAR[5:] + LAST),
+            (all_of(not_up, not_down, qy == 0), give_low, ACROSS[1:]),
+            (all_of(not_up, not_down, qy == 3), give_high, ACROSS[1:]),
+        ),
+    )
+
+    def start_gifts(part):
+        for there, copy, chunks in gifts[part]:
+            start_chunks(there, (copy,), chunks)
 
     sum_start(*late, 0, partial)
     for there, copy, chunks in passes[:4]:
         start_chunks(there, (copy,), chunks)
-    start_chunks(only_low, (give_low,), BESIDE[:2])
-    start_chunks(only_high, (give_high,), BESIDE[:2])
+    start_gifts(0)
     pl.when(lone)(invert)
     partial = sum_end(*late, 0)
     partial = summed(1, partial)
     for there, copy, chunks in passes[4:]:
         start_chunks(there, (copy,), chunks)
     sum_start(*late, 2, partial)
-    start_chunks(not_up, (give_low,), ACROSS[:1])
-    start_chunks(not_down, (give_high,), ACROSS[:1])
+    start_gifts(1)
     total[...] = sum_end(*late, 2)
     hand = remote(total.at[pl.ds(n, n // 2)], prior, prior_send, prior_recv, i + 1, r)
     pl.when(has_next)(lambda: hand.start())
-    start_chunks(not_up, (give_low,), ACROSS[1:])
-    start_chunks(not_down, (give_high,), ACROSS[1:])
-    start_chunks(only_low, (give_low,), BESIDE[2:])
-    start_chunks(only_high, (give_high,), BESIDE[2:])
+    start_gifts(2)
     wait_prior = lambda: pl.when(has_prev)(lambda: hand.wait_recv())
     coefficients(early_total[...], total[...], inv_p[...], prior, wait_prior, w_o, r_o)
 
@@ -476,11 +493,7 @@
     pl.when(has_next)(lambda: early_hand.wait_send())
     end_chunks(has_next, (onward,), range(2 * CHUNKS))
     end_chunks(gives, (give_low, give_high), range(CHUNKS))
-    end_chunks(not_up, (give_low,), ACROSS)
-    end_chunks(not_down, (give_high,), ACROSS)
-    end_chunks(only_low, (give_low,), BESIDE)
-    end_chunks(only_high, (give_high,), BESIDE)
-    for there, copy, chunks in passes:
+    for there, copy, chunks in passes + gifts[0] + gifts[1] + gifts[2]:
         end_chunks(there, (copy,), chunks)
     for there, _, _, copy in first_hops + second_hops:
         pl.when(there)(lambda copy=copy: copy.wait_send())

time: 111 us -> 111 us (level); the launches traced: 109 us -> 111 us
    pallas_call x1, Pallas kernels: 96.3 us -> 97.7 us  [body(): pl.pallas_call(kernel, out_shape=(whole, stack, stack, plane, plane, jax....]
where the time goes in v6:
time: 111 us
  Pallas kernels  107 us (96%)
  local copies, waits for them, and re-layouts  3.02 us (3%)
    pallas_call x1, Pallas kernels, body(): pl.pallas_call(kernel, out_shape=(whole, stack, stack, plane, plane, jax....  97.7 us
    pallas_call x1, Pallas kernels, body(): pl.pallas_call(apply_kernel, out_shape=(whole, jax.ShapeDtypeStruct((n, n...  9.19 us
    unnamed x4, local copies, waits for them, and re-layouts  3.02 us

profile of v6, /device:TPU:62, one launch (start us, length us, event | category | flops | bytes accessed | tf_op | source)
XLA Modules:
  0.0 110.6 jit_solution(152505927640239222)
XLA Ops:
  0.6 0.0 copy-start
  0.6 2.2 %copy-done = f32[1,64,16384]{2,1,0:T(8,128)S(1)} copy-done((f32[1,64,16384]{2,1,0:T(8,128)S(1)}, f32[1,64,16384]{2,1,0:T(8,128)}, u32[]{:S(2)}) %copy-start) | copy-done | bytes 4194328
  2.8 0.0 copy-start.1
  2.8 0.8 copy-done.1
  3.7 97.7 %exchange.1 = (f32[64,16384]{1,0:T(8,128)S(1)}, bf16[192,16384]{1,0:T(8,128)(2,1)S(1)}, bf16[192,16384]{1,0:T(8,128)(2,1)S(1)}, f32[64,8192]{1,0:T(8,128)S(1)}, ...) custom-call(f32[64,16384]{1,0:T(8,128)S(1)} %bitcast.5, f32[1,16384]{1,0:T(1,128)S(1)} %bitcast.6), custom_call_target="tpu_custom_call" | custom-call | tf_op jit(solution)/shard_map/exchange/pallas_call | solution.py:576
  101.4 9.2 %apply.1 = (f32[64,16384]{1,0:T(8,128)}, f32[64,64]{1,0:T(8,128)}, f32[64,16384]{1,0:T(8,128)}) custom-call(f32[64,16384]{1,0:T(8,128)S(1)} %get-tuple-element.13.prev, bf16[192,16384]{1,0:T(8,128)(2,1)S(1)} %get-tuple-element.14.z_hi, bf16[192,16384]{1,0:T(8,128)(2,1)S(1)} %get-tuple-element.15.z_lo, f32[64,8192]{1,0:T(8,128)S(1)} %get-tuple-element.16.plow, ...), custom_call_target="tpu_custom_call" | custom-call | tf_op jit(solution)/shard_map/apply/pallas_call | solution.py:612
Async XLA Ops:
  0.6 2.2 %copy-start = (f32[1,64,16384]{2,1,0:T(8,128)S(1)}, f32[1,64,16384]{2,1,0:T(8,128)}, u32[]{:S(2)}) copy-start(f32[1,64,16384]{2,1,0:T(8,128)} %param.2) | copy-start | bytes 12582916
  2.8 0.8 copy-start.1

commit v7 on v6

--- a/solution.py
+++ b/solution.py
@@ -208,10 +208,6 @@
     early = (early_sums, early_send, early_recv)
     late = (sums, sum_send, sum_recv)
 
-    def summed(stage, value):
-        sum_start(*late, stage, value)
-        return sum_end(*late, stage)
-
     sum_start(*early, 0, own_gram)
 
     last_of_layer, first_of_layer = q == LAYER - 1, q == 0
@@ -464,9 +460,10 @@
     start_gifts(0)
     pl.when(lone)(invert)
     partial = sum_end(*late, 0)
-    partial = summed(1, partial)
+    sum_start(*late, 1, partial)
     for there, copy, chunks in passes[4:]:
         start_chunks(there, (copy,), chunks)
+    partial = sum_end(*late, 1)
     sum_start(*late, 2, partial)
     start_gifts(1)
     total[...] = sum_end(*late, 2)

time: 111 us -> 116 us (1.045); the launches traced: 111 us -> 114 us
  Pallas kernels: 107 us -> 110 us
    pallas_call x1, Pallas kernels: 97.7 us -> 101 us  [body(): pl.pallas_call(kernel, out_shape=(whole, stack, stack, plane, plane, jax....]
where the time goes in v7:
time: 116 us; the launch traced here: 114 us
  Pallas kernels  110 us (95%)
  local copies, waits for them, and re-layouts  3.02 us (3%)
    pallas_call x1, Pallas kernels, body(): pl.pallas_call(kernel, out_shape=(whole, stack, stack, plane, plane, jax....  101 us
    pallas_call x1, Pallas kernels, body(): pl.pallas_call(apply_kernel, out_shape=(whole, jax.ShapeDtypeStruct((n, n...  9.2 us
    unnamed x4, local copies, waits for them, and re-layouts  3.02 us

profile of v7, /device:TPU:62, one launch (start us, length us, event | category | flops | bytes accessed | tf_op | source)
XLA Modules:
  0.0 114.1 jit_solution(18047918424398899967)
XLA Ops:
  0.6 0.0 copy-start
  0.6 2.2 %copy-done = f32[1,64,16384]{2,1,0:T(8,128)S(1)} copy-done((f32[1,64,16384]{2,1,0:T(8,128)S(1)}, f32[1,64,16384]{2,1,0:T(8,128)}, u32[]{:S(2)}) %copy-start) | copy-done | bytes 4194328
  2.8 0.0 copy-start.1
  2.8 0.8 copy-done.1
  3.7 101.2 %exchange.1 = (f32[64,16384]{1,0:T(8,128)S(1)}, bf16[192,16384]{1,0:T(8,128)(2,1)S(1)}, bf16[192,16384]{1,0:T(8,128)(2,1)S(1)}, f32[64,8192]{1,0:T(8,128)S(1)}, ...) custom-call(f32[64,16384]{1,0:T(8,128)S(1)} %bitcast.5, f32[1,16384]{1,0:T(1,128)S(1)} %bitcast.6), custom_call_target="tpu_custom_call" | custom-call | tf_op jit(solution)/shard_map/exchange/pallas_call | solution.py:573
  104.9 9.2 %apply.1 = (f32[64,16384]{1,0:T(8,128)}, f32[64,64]{1,0:T(8,128)}, f32[64,16384]{1,0:T(8,128)}) custom-call(f32[64,16384]{1,0:T(8,128)S(1)} %get-tuple-element.13.prev, bf16[192,16384]{1,0:T(8,128)(2,1)S(1)} %get-tuple-element.14.z_hi, bf16[192,16384]{1,0:T(8,128)(2,1)S(1)} %get-tuple-element.15.z_lo, f32[64,8192]{1,0:T(8,128)S(1)} %get-tuple-element.16.plow, ...), custom_call_target="tpu_custom_call" | custom-call | tf_op jit(solution)/shard_map/apply/pallas_call | solution.py:609
Async XLA Ops:
  0.6 2.2 %copy-start = (f32[1,64,16384]{2,1,0:T(8,128)S(1)}, f32[1,64,16384]{2,1,0:T(8,128)}, u32[]{:S(2)}) copy-start(f32[1,64,16384]{2,1,0:T(8,128)} %param.2) | copy-start | bytes 12582916
  2.8 0.8 copy-start.1
